TPU v7x, 8 devices: a whole 2x2x1 slice. The times are simulated.
8 devices in a mesh: batch: 1 (over z), pcol: 2 (over y), prow: 4 (over x, core).
Axes of the slice: x: 2, y: 2, z: 1, core: 2. Of those that a mesh axis runs over, the one named last changes fastest.
Arguments:
- a_mat: float32 [24576, 1024], P(('batch', 'prow'), 'pcol')
- diag_shift: float32 [4, 128], P('batch')
Outputs:
- output: float32 [512, 1024], P('batch', 'pcol')
All inputs are finite; a program needn't handle non-finite values.
Results may differ from a plain program's by a relative error of at most 0.001.
Values sent between devices are 32-bit elements.
A program may use at most 1 GiB of HBM per device.

v0:
```python
import jax
import jax.numpy as jnp
from jax import lax
from jax.sharding import PartitionSpec as P

PRECISE = lax.Precision.HIGHEST


def factor_panel(panel, glob_rows, col_base):
    blocksize = panel.shape[1]
    lane_ids = jnp.arange(blocksize)

    def col_step(k, loop_state):
        panel, vectors, tau_vec, sign_vec = loop_state
        glob_col = col_base + k
        active = glob_rows >= glob_col
        is_pivot = glob_rows == glob_col
        column = lax.dynamic_slice_in_dim(panel, k, 1, axis=1)[:, 0]
        stacked = jnp.stack([jnp.where(active, column, 0.0), is_pivot.astype(jnp.float32)])
        reduced = lax.psum(jnp.dot(stacked, panel, precision=PRECISE, preferred_element_type=jnp.float32), 'prow')
        col_dots = reduced[0]
        pivot_row = reduced[1]
        pivot_val = lax.dynamic_index_in_dim(pivot_row, k, keepdims=False)
        col_norm = jnp.sqrt(lax.dynamic_index_in_dim(col_dots, k, keepdims=False))
        beta_val = jnp.where(pivot_val >= 0, -col_norm, col_norm)
        tau_val = (beta_val - pivot_val) / beta_val
        inv_scale = 1.0 / (pivot_val - beta_val)
        v_col = jnp.where(is_pivot, 1.0, jnp.where(active, column * inv_scale, 0.0))
        v_dots = inv_scale * (col_dots - pivot_val * pivot_row) + pivot_row
        update = jnp.where(lane_ids > k, tau_val * v_dots, 0.0)
        new_col = jnp.where(active, jnp.where(is_pivot, beta_val, 0.0), column)
        panel = panel - v_col[:, None] * update[None, :]
        panel = lax.dynamic_update_slice_in_dim(panel, new_col[:, None], k, axis=1)
        vectors = lax.dynamic_update_slice_in_dim(vectors, v_col[:, None], k, axis=1)
        tau_vec = jnp.where(lane_ids == k, tau_val, tau_vec)
        sign_vec = jnp.where(lane_ids == k, jnp.where(beta_val < 0, -1.0, 1.0), sign_vec)
        return panel, vectors, tau_vec, sign_vec

    init_state = (panel, jnp.zeros_like(panel), jnp.zeros((blocksize,), jnp.float32), jnp.zeros((blocksize,), jnp.float32))
    return lax.fori_loop(0, blocksize, col_step, init_state)


def build_tfactor(gram_mat, tau_vec):
    blocksize = tau_vec.shape[0]
    lane_ids = jnp.arange(blocksize)

    def t_step(k, t_factor):
        gram_col = jnp.where(lane_ids < k, lax.dynamic_slice_in_dim(gram_mat, k, 1, axis=1)[:, 0], 0.0)
        tau_k = lax.dynamic_index_in_dim(tau_vec, k, keepdims=False)
        column = -tau_k * jnp.dot(t_factor, gram_col, precision=PRECISE, preferred_element_type=jnp.float32)
        column = jnp.where(lane_ids == k, tau_k, column)
        return jnp.where(lane_ids[None, :] == k, column[:, None], t_factor)

    return lax.fori_loop(0, blocksize, t_step, jnp.zeros((blocksize, blocksize), jnp.float32))


def solution(mesh):
    n_pcol = mesh.shape['pcol']

    def local_qr(a_loc, diag_shift):
        rows_loc, cols_loc = a_loc.shape
        panels, blocksize = diag_shift.shape
        total_k = panels * blocksize
        row_id = lax.axis_index('prow')
        col_id = lax.axis_index('pcol')
        glob_rows = row_id * rows_loc + jnp.arange(rows_loc)
        local_cols = jnp.arange(cols_loc)
        orig_cols = ((local_cols // blocksize) * n_pcol + col_id) * blocksize + local_cols % blocksize
        shift_flat = diag_shift.reshape(total_k)
        col_shift = jnp.where(orig_cols < total_k, shift_flat[jnp.minimum(orig_cols, total_k - 1)], 0.0)
        diag_hit = (jnp.arange(total_k)[:, None] == orig_cols[None, :]) & (row_id == 0)
        a_loc = a_loc.at[:total_k].add(jnp.where(diag_hit, col_shift[None, :], 0.0))
        sign_parts = []
        for panel_idx in range(panels):
            owner_col = panel_idx % n_pcol
            start_col = (panel_idx // n_pcol) * blocksize
            is_owner = col_id == owner_col
            factored, vectors, tau_vec, sign_vec = factor_panel(a_loc[:, start_col:start_col + blocksize], glob_rows, panel_idx * blocksize)
            gram_mat = lax.psum(jnp.einsum('mi,mj->ij', vectors, vectors, precision=PRECISE, preferred_element_type=jnp.float32), 'prow')
            t_factor = build_tfactor(gram_mat, tau_vec)
            vectors, t_factor, sign_vec = lax.psum((jnp.where(is_owner, vectors, 0.0), jnp.where(is_owner, t_factor, 0.0), jnp.where(is_owner, sign_vec, 0.0)), 'pcol')
            sign_parts.append(sign_vec)
            trailing = a_loc[:, start_col:]
            keep_cols = (jnp.arange(cols_loc - start_col) >= blocksize) | (col_id > owner_col)
            proj_sum = lax.psum(jnp.einsum('mi,mn->in', vectors, trailing, precision=PRECISE, preferred_element_type=jnp.float32), 'prow')
            w_mat = jnp.where(keep_cols[None, :], jnp.einsum('ij,in->jn', t_factor, proj_sum, precision=PRECISE, preferred_element_type=jnp.float32), 0.0)
            trailing = trailing - jnp.dot(vectors, w_mat, precision=PRECISE, preferred_element_type=jnp.float32)
            trailing = trailing.at[:, :blocksize].set(jnp.where(is_owner, factored, trailing[:, :blocksize]))
            a_loc = a_loc.at[:, start_col:].set(trailing)
        all_signs = jnp.concatenate(sign_parts)
        top_rows = lax.psum(jnp.where(row_id == 0, a_loc[:total_k], 0.0), 'prow')
        return top_rows * all_signs[:, None]

    return jax.shard_map(local_qr, mesh=mesh, in_specs=(P(('batch', 'prow'), 'pcol'), P('batch', None)), out_specs=P('batch', 'pcol'), check_vma=False)
```

profile of v0, /device:TPU:0, one launch (start us, length us, event | category | flops | bytes accessed | tf_op | source)
XLA Modules:
  0.0 10875.0 jit_solution(1045559057514553981)
XLA Ops:
  6.5 10.6 copy.140
  31.3 2161.2 %while.155 = (s32[]{:T(128)}, f32[6144,128]{0,1:T(8,128)S(1)}, f32[6144,128]{0,1:T(8,128)}, f32[128]{0:T(128)S(1)}, f32[128]{0:T(128)S(1)}, /*index=5*/s32[]{:T(...) while((s32[]{:T(128)}, f32[6144,128]{0,1:T(8,128)S(1)}, ...), condition=%wide.region_2.3_spmd.clone.clone, body=%wide.region_0.2_spmd.clone.clone.sunk | while | flops 20535168 | bytes 9796932 | solution.py:40
  33.9 8.7 psum.224
  103.3 6.4 psum.224
  204.3 6.5 psum.224
  744.0 6.5 psum.224
  845.2 6.5 psum.224
  1807.0 6.5 psum.224
  1908.0 6.4 psum.224
  2206.4 73.0 all-reduce.19.cloned.1.call-done
  2279.4 14.7 fusion.146
  2297.4 23.9 all-reduce.43.cloned.1.call-done
  2321.3 372.0 %while.156 = (s32[]{:T(128)}, f32[128,128]{1,0:T(8,128)S(1)}, f32[128]{0:T(128)S(1)}, f32[128,128]{0,1:T(8,128)}, s32[]{:T(128)}, /*index=5*/s32[]{:T(128)}) while((s32[]{:T(128)}, f32[128,128]{1,0:T(8,128)S(1)}, f32[128]{0:T(128)S(1)}, f32[128,128]{0,1:T(8,128)}, s32[]{:T(128)}, /*index=5*/s32[]{:T(128)}) %tuple.332), condition=%wide.region_6.7_spmd.clone.clone, body=%wide.region_5.6_spmd.clone.clone.sunk | while | flops 246532 | bytes 201583 | solution.py:54
  2694.6 14.9 all-reduce.21.cloned.1.call-done
  2710.9 13.6 convolution_subtract_fusion.1
  2736.9 2149.4 %while.157 = (s32[]{:T(128)}, f32[6144,128]{0,1:T(8,128)S(1)}, f32[6144,128]{0,1:T(8,128)}, f32[128]{0:T(128)S(1)}, f32[128]{0:T(128)S(1)}, /*index=5*/s32[]{:T(...) while((s32[]{:T(128)}, f32[6144,128]{0,1:T(8,128)S(1)}, ...), condition=%wide.region_12.13_spmd.clone.clone, body=%wide.region_10.12_spmd.clone.clone.sunk | while | flops 20535172 | bytes 9796952 | solution.py:40
  4452.8 6.4 psum.225
  4553.6 6.3 psum.225
  4620.4 6.3 psum.225
  4721.3 6.3 psum.225
  4822.1 6.4 psum.225
  4898.2 74.7 all-reduce.23.cloned.1.call-done
  4972.9 14.7 fusion.148
  4987.7 27.0 all-reduce.41.cloned.1.call-done
  5014.7 372.1 %while.158 = (s32[]{:T(128)}, f32[128,128]{1,0:T(8,128)S(1)}, f32[128]{0:T(128)S(1)}, f32[128,128]{0,1:T(8,128)}, s32[]{:T(128)}, /*index=5*/s32[]{:T(128)}) while((s32[]{:T(128)}, f32[128,128]{1,0:T(8,128)S(1)}, f32[128]{0:T(128)S(1)}, f32[128,128]{0,1:T(8,128)}, s32[]{:T(128)}, /*index=5*/s32[]{:T(128)}) %tuple.338), condition=%wide.region_16.17_spmd.clone.clone, body=%wide.region_15.16_spmd.clone.clone.sunk | while | flops 246532 | bytes 201583 | solution.py:54
  5390.1 12.8 all-reduce.25.cloned.1.call-done
  5404.2 13.6 convolution_subtract_fusion
  5430.4 2149.0 %while.159 = (s32[]{:T(128)}, f32[6144,128]{0,1:T(8,128)S(1)}, f32[6144,128]{0,1:T(8,128)}, f32[128]{0:T(128)S(1)}, f32[128]{0:T(128)S(1)}, /*index=5*/s32[]{:T(...) while((s32[]{:T(128)}, f32[6144,128]{0,1:T(8,128)S(1)}, ...), condition=%wide.region_21.22_spmd.clone.clone, body=%wide.region_19.21_spmd.clone.clone.sunk | while | flops 20535172 | bytes 9796952 | solution.py:40
  6239.1 6.4 psum.226
  6340.0 6.3 psum.226
  6406.9 6.3 psum.226
  6507.7 6.3 psum.226
  6608.5 6.4 psum.226
  6675.3 6.4 psum.226
  6776.2 6.3 psum.226
  7045.0 6.4 psum.226
  7145.9 6.3 psum.226
  7212.7 6.3 psum.226
  7313.5 6.3 psum.226
  7414.3 6.4 psum.226
  7481.2 6.4 psum.226
  7593.4 73.5 all-reduce.27.cloned.1.call-done
  7666.9 12.0 fusion.112
  7679.6 26.1 all-reduce.39.cloned.1.call-done
  7705.7 372.1 %while.160 = (s32[]{:T(128)}, f32[128,128]{1,0:T(8,128)S(1)}, f32[128]{0:T(128)S(1)}, f32[128,128]{0,1:T(8,128)}, s32[]{:T(128)}, /*index=5*/s32[]{:T(128)}) while((s32[]{:T(128)}, f32[128,128]{1,0:T(8,128)S(1)}, f32[128]{0:T(128)S(1)}, f32[128,128]{0,1:T(8,128)}, s32[]{:T(128)}, /*index=5*/s32[]{:T(128)}) %tuple.344), condition=%wide.region_25.26_spmd.clone.clone, body=%wide.region_24.25_spmd.clone.clone.sunk | while | flops 246532 | bytes 201583 | solution.py:54
  8081.1 12.9 all-reduce.29.cloned.1.call-done
  8095.2 11.1 convolution_subtract_fusion.3
  8117.6 2177.3 %while.161 = (s32[]{:T(128)}, f32[6144,128]{0,1:T(8,128)S(1)}, f32[6144,128]{0,1:T(8,128)}, f32[128]{0:T(128)S(1)}, f32[128]{0:T(128)S(1)}, /*index=5*/s32[]{:T(...) while((s32[]{:T(128)}, f32[6144,128]{0,1:T(8,128)S(1)}, ...), condition=%wide.region_31.32_spmd.clone.clone, body=%wide.region_29.31_spmd.clone.clone.sunk | while | flops 20535172 | bytes 9796952 | solution.py:40
  8936.6 6.4 psum.227
  9209.0 6.3 psum.227
  9311.2 6.4 psum.227
  9378.9 6.4 psum.227
  9481.2 6.3 psum.227
  9753.0 6.4 psum.227
  10025.4 6.3 psum.227
  10127.6 6.4 psum.227
  10195.4 6.4 psum.227
  10306.9 75.0 all-reduce.31.cloned.1.call-done
  10381.9 12.0 fusion.151
  10394.0 26.8 all-reduce.37.cloned.1.call-done
  10420.8 372.0 %while.162 = (s32[]{:T(128)}, f32[128,128]{1,0:T(8,128)S(1)}, f32[128]{0:T(128)S(1)}, f32[128,128]{0,1:T(8,128)}, s32[]{:T(128)}, /*index=5*/s32[]{:T(128)}) while((s32[]{:T(128)}, f32[128,128]{1,0:T(8,128)S(1)}, f32[128]{0:T(128)S(1)}, f32[128,128]{0,1:T(8,128)}, s32[]{:T(128)}, /*index=5*/s32[]{:T(128)}) %tuple.350), condition=%wide.region_35.36_spmd.clone.clone, body=%wide.region_34.35_spmd.clone.clone.sunk | while | flops 246532 | bytes 201583 | solution.py:54
  10793.8 8.0 constant_dynamic-update-slice_fusion.1
  10810.3 13.2 convolution_subtract_fusion.2
  10839.9 26.0 all-reduce.35.cloned.1.call-done
  (9823 shorter events, 7988.2 us)
Async XLA Ops:
  6.5 10.7 copy-start
  6.5 2272.9 %all-reduce.19.cloned.1.call-start = ((), (), s32[]{:S(2)}) async-start(), calls=%async_computation | async-start | bytes 6291456 | tf_op jit(solution)/shard_map/psum | solution.py:81
  2200.0 121.3 %all-reduce.43.cloned.1.call-start = ((), (), s32[]{:S(2)}) async-start(), calls=%async_computation.12 | async-start | bytes 655360 | tf_op jit(solution)/shard_map/psum | solution.py:79
  2294.2 415.2 %all-reduce.21.cloned.1.call-start = ((), (), s32[]{:S(2)}) async-start(), calls=%async_computation.1 | async-start | bytes 131072 | tf_op jit(solution)/shard_map/psum | solution.py:81
  2694.0 2278.9 %all-reduce.23.cloned.1.call-start = ((), (), s32[]{:S(2)}) async-start(), calls=%async_computation.2 | async-start | bytes 6291456 | tf_op jit(solution)/shard_map/psum | solution.py:81
  2710.9 13.6 copy-start.7
  2728.0 4.5 copy-start.3
  4891.8 122.9 %all-reduce.41.cloned.1.call-start = ((), (), s32[]{:S(2)}) async-start(), calls=%async_computation.11 | async-start | bytes 655360 | tf_op jit(solution)/shard_map/psum | solution.py:79
  4987.7 415.3 %all-reduce.25.cloned.1.call-start = ((), (), s32[]{:S(2)}) async-start(), calls=%async_computation.3 | async-start | bytes 131072 | tf_op jit(solution)/shard_map/psum | solution.py:81
  5387.5 2279.4 %all-reduce.27.cloned.1.call-start = ((), (), s32[]{:S(2)}) async-start(), calls=%async_computation.4 | async-start | bytes 6291456 | tf_op jit(solution)/shard_map/psum | solution.py:81
  5387.7 15.2 copy-start.9
  5404.2 13.6 copy-start.5
  5419.4 4.5 copy-start.4
  7586.8 118.9 %all-reduce.39.cloned.1.call-start = ((), (), s32[]{:S(2)}) async-start(), calls=%async_computation.10 | async-start | bytes 524288 | tf_op jit(solution)/shard_map/psum | solution.py:79
  7678.9 415.0 %all-reduce.29.cloned.1.call-start = ((), (), s32[]{:S(2)}) async-start(), calls=%async_computation.5 | async-start | bytes 131072 | tf_op jit(solution)/shard_map/psum | solution.py:81
  8078.5 2303.4 %all-reduce.31.cloned.1.call-start = ((), (), s32[]{:S(2)}) async-start(), calls=%async_computation.6 | async-start | bytes 6291456 | tf_op jit(solution)/shard_map/psum | solution.py:81
  8078.7 15.2 copy-start.10
  8095.1 11.1 copy-start.8
  8109.6 3.6 copy-start.2
  10300.4 120.3 %all-reduce.37.cloned.1.call-start = ((), (), s32[]{:S(2)}) async-start(), calls=%async_computation.9 | async-start | bytes 524288 | tf_op jit(solution)/shard_map/psum | solution.py:79
  10393.9 415.0 %all-reduce.33.cloned.1.call-start = ((), (), s32[]{:S(2)}) async-start(), calls=%async_computation.7 | async-start | bytes 131072 | tf_op jit(solution)/shard_map/psum | solution.py:81
  10793.5 72.4 all-reduce.35.cloned.1.call-start
  10801.8 7.2 copy-start.11
  10808.9 19.2 slice-start
  10810.3 13.3 copy-start.6
  10810.3 17.8 slice-start.1
  10810.3 17.8 slice-start.2
  10828.1 40.1 copy-start.1
Sparse Core Ops, SparseCore 0:
  2200.1 79.3 all-reduce.18
  2294.3 26.9 all-reduce.42
  2694.1 15.2 all-reduce.20
  4891.9 80.8 all-reduce.22
  4987.8 26.9 all-reduce.40
  5387.6 15.2 all-reduce.24
  7586.9 79.8 all-reduce.26
  7679.0 26.6 all-reduce.38
  8078.6 15.2 all-reduce.28
  10300.6 81.2 all-reduce.30
  10394.0 26.6 all-reduce.36
  10793.6 15.2 all-reduce.32
  10835.0 30.8 all-reduce.34
where the time goes:
time: 11000 us; the launch traced here: 10900 us
  blocking collectives  3060 us (28%)
  matrix products  2200 us (20%)
  local copies, waits for them, and re-layouts  2190 us (20%)
  loops' own time  2060 us (19%)
  other arithmetic  870 us (8%)
  waiting for transfers between devices  471 us (4%)
    psum x512, blocking collectives, col_step(): lax.psum(jnp.dot(stacked, panel, precision=PRECISE, preferred_element_typ...  3060 us
    another operation x4, loops' own time, factor_panel(): return lax.fori_loop(0, blocksize, col_step, init_state)  1710 us
    dot_general x512, matrix products, col_step(): jnp.dot(stacked, panel, precision=PRECISE, preferred_element_type=jnp.flo...  1290 us
    dynamic_update_slice x512, local copies, waits for them, and re-layouts, col_step(): lax.dynamic_update_slice_in_dim(vectors, v_col[:, None], k, axis=1)  870 us
    dot_general x512, matrix products, t_step(): jnp.dot(t_factor, gram_col, precision=PRECISE, preferred_element_type=jnp...  767 us
    another operation x4, loops' own time, build_tfactor(): lax.fori_loop(0, blocksize, t_step, jnp.zeros((blocksize, blocksize), jnp...  351 us
    psum x8, waiting for transfers between devices, local_qr(): lax.psum((jnp.where(is_owner, vectors, 0.0), jnp.where(is_owner, t_factor...  341 us
    mul x512, other arithmetic, col_step(): panel = panel - v_col[:, None] * update[None, :]  339 us

commit v1 on v0

v1 whole, which is shorter than its diff:
```python
import functools

import jax
import jax.numpy as jnp
from jax import lax
from jax.experimental import pallas as pl
from jax.experimental.pallas import tpu as pltpu
from jax.sharding import PartitionSpec as P

PRECISE = lax.Precision.HIGHEST
F32 = jnp.float32
NB = 128
MESH = pl.DeviceIdType.MESH
TRACE_FACTOR = 2.0


def dot_nn(x, y):
    return lax.dot_general(x, y, (((1,), (0,)), ((), ())), precision=PRECISE, preferred_element_type=F32)


def dot_tn(x, y):
    return lax.dot_general(x, y, (((0,), (0,)), ((), ())), precision=PRECISE, preferred_element_type=F32)


def gather_sum(x, axis):
    return jnp.sum(lax.all_gather(x, axis), axis=0)


def factor_panel(panel, glob_rows, col_base):
    blocksize = panel.shape[1]
    lane_ids = jnp.arange(blocksize)

    def col_step(k, loop_state):
        panel, vectors, tau_vec, sign_vec = loop_state
        glob_col = col_base + k
        active = glob_rows >= glob_col
        is_pivot = glob_rows == glob_col
        column = lax.dynamic_slice_in_dim(panel, k, 1, axis=1)[:, 0]
        reduced = gather_sum(jnp.stack([jnp.sum(jnp.where(active, column, 0.0)[:, None] * panel, axis=0),
                                        jnp.sum(jnp.where(is_pivot[:, None], panel, 0.0), axis=0)]), 'prow')
        col_dots = reduced[0]
        pivot_row = reduced[1]
        pivot_val = lax.dynamic_index_in_dim(pivot_row, k, keepdims=False)
        col_norm = jnp.sqrt(lax.dynamic_index_in_dim(col_dots, k, keepdims=False))
        beta_val = jnp.where(pivot_val >= 0, -col_norm, col_norm)
        tau_val = (beta_val - pivot_val) / beta_val
        inv_scale = 1.0 / (pivot_val - beta_val)
        v_col = jnp.where(is_pivot, 1.0, jnp.where(active, column * inv_scale, 0.0))
        v_dots = inv_scale * (col_dots - pivot_val * pivot_row) + pivot_row
        update = jnp.where(lane_ids > k, tau_val * v_dots, 0.0)
        new_col = jnp.where(active, jnp.where(is_pivot, beta_val, 0.0), column)
        panel = panel - v_col[:, None] * update[None, :]
        panel = lax.dynamic_update_slice_in_dim(panel, new_col[:, None], k, axis=1)
        vectors = lax.dynamic_update_slice_in_dim(vectors, v_col[:, None], k, axis=1)
        tau_vec = jnp.where(lane_ids == k, tau_val, tau_vec)
        sign_vec = jnp.where(lane_ids == k, jnp.where(beta_val < 0, -1.0, 1.0), sign_vec)
        return panel, vectors, tau_vec, sign_vec

    init_state = (panel, jnp.zeros_like(panel), jnp.zeros((blocksize,), F32), jnp.zeros((blocksize,), F32))
    return lax.fori_loop(0, blocksize, col_step, init_state)


def build_tfactor(gram_mat, tau_vec):
    blocksize = tau_vec.shape[0]
    lane_ids = jnp.arange(blocksize)

    def t_step(k, t_factor):
        gram_col = jnp.where(lane_ids < k, lax.dynamic_slice_in_dim(gram_mat, k, 1, axis=1)[:, 0], 0.0)
        tau_k = lax.dynamic_index_in_dim(tau_vec, k, keepdims=False)
        column = -tau_k * jnp.sum(t_factor * gram_col[None, :], axis=1)
        column = jnp.where(lane_ids == k, tau_k, column)
        return jnp.where(lane_ids[None, :] == k, column[:, None], t_factor)

    return lax.fori_loop(0, blocksize, t_step, jnp.zeros((blocksize, blocksize), F32))


def householder_rows(a_loc, diag_shift, n_pcol):
    rows_loc, cols_loc = a_loc.shape
    panels, blocksize = diag_shift.shape
    total_k = panels * blocksize
    row_id = lax.axis_index('prow')
    col_id = lax.axis_index('pcol')
    glob_rows = row_id * rows_loc + jnp.arange(rows_loc)
    local_cols = jnp.arange(cols_loc)
    orig_cols = ((local_cols // blocksize) * n_pcol + col_id) * blocksize + local_cols % blocksize
    shift_flat = diag_shift.reshape(total_k)
    col_shift = jnp.where(orig_cols < total_k, shift_flat[jnp.minimum(orig_cols, total_k - 1)], 0.0)
    a_loc = a_loc + jnp.where(glob_rows[:, None] == orig_cols[None, :], col_shift[None, :], 0.0)
    swap = [(0, 1), (1, 0)]

    def owned(x, is_owner):
        return jnp.where(is_owner, x, lax.ppermute(x, 'pcol', swap))

    def panel_step(panel_idx, state):
        a_loc, signs = state
        owner_col = panel_idx % n_pcol
        start_col = (panel_idx // n_pcol) * blocksize
        is_owner = col_id == owner_col
        panel = lax.dynamic_slice_in_dim(a_loc, start_col, blocksize, axis=1)
        factored, vectors, tau_vec, sign_vec = factor_panel(panel, glob_rows, panel_idx * blocksize)
        gram_mat = gather_sum(jnp.einsum('mi,mj->ij', vectors, vectors, precision=PRECISE, preferred_element_type=F32), 'prow')
        t_factor = build_tfactor(gram_mat, tau_vec)
        vectors, t_factor, sign_vec = owned(vectors, is_owner), owned(t_factor, is_owner), owned(sign_vec, is_owner)
        signs = lax.dynamic_update_slice_in_dim(signs, sign_vec, panel_idx * blocksize, axis=0)
        keep_cols = orig_cols >= (panel_idx + 1) * blocksize
        proj = jnp.einsum('mi,mn->in', vectors, a_loc, precision=PRECISE, preferred_element_type=F32)
        quarter = cols_loc // 4
        proj_sum = jnp.concatenate([gather_sum(proj[:, q * quarter:(q + 1) * quarter], 'prow') for q in range(4)], axis=1)
        w_mat = jnp.where(keep_cols[None, :], jnp.einsum('ij,in->jn', t_factor, proj_sum, precision=PRECISE, preferred_element_type=F32), 0.0)
        a_loc = a_loc - jnp.dot(vectors, w_mat, precision=PRECISE, preferred_element_type=F32)
        kept = lax.dynamic_slice_in_dim(a_loc, start_col, blocksize, axis=1)
        a_loc = lax.dynamic_update_slice_in_dim(a_loc, jnp.where(is_owner, factored, kept), start_col, axis=1)
        return a_loc, signs

    a_loc, signs = lax.fori_loop(0, panels, panel_step, (a_loc, jnp.zeros((total_k,), F32)))
    step = total_k // 8

    def top_step(i, top):
        piece = lax.all_gather(lax.dynamic_slice_in_dim(a_loc, i * step, step, axis=0), 'prow')[0]
        return lax.dynamic_update_slice_in_dim(top, piece, i * step, axis=0)

    top_rows = lax.fori_loop(0, 8, top_step, jnp.zeros((total_k, cols_loc), F32))
    return top_rows * signs[:, None]


def factor_block(block, u_ref, m_ref):
    sub = lax.broadcasted_iota(jnp.int32, (8, NB), 0)
    lane = lax.broadcasted_iota(jnp.int32, (8, NB), 1)
    eye = (lax.broadcasted_iota(jnp.int32, (NB, NB), 0) == lax.broadcasted_iota(jnp.int32, (NB, NB), 1)).astype(F32)

    def group(g, state):
        s_mat, m_mat = state
        for t in range(8):
            row_s = s_mat[t:t + 1, :]
            row_m = m_mat[t:t + 1, :]
            inv_p = 1.0 / s_mat[t:t + 1, t:t + 1]
            row_s = row_s * inv_p
            row_m = row_m * inv_p
            col = s_mat[:, t:t + 1]
            top = jnp.where(sub[:, 0:1] > t, col[:8], 0.0)
            col = jnp.concatenate([top, col[8:]], axis=0)
            s_mat = s_mat - col * row_s
            m_mat = m_mat - col * row_m
        s_top, m_top = s_mat[:8], m_mat[:8]
        diag = jnp.sum(jnp.where(lane == sub, s_top, 0.0), axis=1, keepdims=True)
        scale = 1.0 / jnp.sqrt(diag)
        base = pl.multiple_of(g * 8, 8)
        u_top = pltpu.roll(jnp.where(lane >= sub, s_top * scale, 0.0), base, 1)
        u_ref[pl.ds(base, 8), :] = jnp.where(lane >= sub + base, u_top, 0.0)
        m_ref[pl.ds(base, 8), :] = m_top * scale
        zero = jnp.zeros((8, NB), F32)
        s_mat = pltpu.roll(jnp.concatenate([s_mat[8:], zero], axis=0), NB - 8, 1)
        m_mat = jnp.concatenate([m_mat[8:], zero], axis=0)
        return s_mat, m_mat

    lax.fori_loop(0, NB // 8, group, (block, eye))


def gram_kernel(a_hbm, s_ref, r_hbm, ok_ref, w_buf, y_buf, acc1, acc2, acc1_r, h_buf, cm_buf, cm_recv, cy_recv, cfin,
                xp, xp_r, z_buf, t_buf, rf_buf, k12, r_buf, ymax, u_blk, m_blk,
                load_sem, ya_send, ya_recv, yb_send, yb_recv, ar_send, ar_recv, gy_send, gy_recv, gq_send, gq_recv,
                rs_send, rs_recv, cy_send, cy_rsem, ag_send, ag_recv, out_sem):
    rows, cols = a_hbm.shape
    half_rows = rows // 2
    half = cols // 2
    kk = 2 * half
    c = lax.axis_index('pcol')
    p = lax.axis_index('prow')
    other = 1 - c
    core_peer = p + 1 - 2 * (p % 2)
    x_peer = (p + 2) % 4
    qr = half // 4
    ca = 512
    n_a = half_rows // ca
    cb = 768
    n_b = half_rows // cb
    n_l = rows // ca

    def row0(start, size):
        return pl.ds(pl.multiple_of(start, NB), size)

    def load(j):
        rs = pl.ds(pl.multiple_of(j * ca, ca), ca)
        return (pltpu.make_async_copy(a_hbm.at[rs, pl.ds(0, half)], w_buf.at[c, rs, :], load_sem.at[0, j]),
                pltpu.make_async_copy(a_hbm.at[rs, pl.ds(half, half)], y_buf.at[rs, :], load_sem.at[1, j]))

    for j in range(n_l):
        for cp in load(j):
            cp.start()

    barrier = pltpu.get_barrier_semaphore()
    pl.semaphore_signal(barrier, inc=1, device_id={'pcol': other}, device_id_type=MESH)
    for d in range(1, 4):
        pl.semaphore_signal(barrier, inc=1, device_id={'prow': (p + d) % 4}, device_id_type=MESH)
    pl.semaphore_wait(barrier, 4)

    def send_a(k):
        rs = row0(c * half_rows + k * ca, ca)
        return pltpu.make_async_remote_copy(a_hbm.at[rs, pl.ds(0, half)], w_buf.at[c, rs, :], ya_send.at[k], ya_recv.at[k],
                                            device_id={'pcol': other}, device_id_type=MESH)

    def send_b(l, k):
        rs = row0(other * half_rows + k * cb, cb)
        ls = pl.ds(l * NB, NB)
        return pltpu.make_async_remote_copy(a_hbm.at[rs, ls], w_buf.at[c, rs, ls], yb_send.at[l, k], yb_recv.at[l, k],
                                            device_id={'pcol': other}, device_id_type=MESH)

    for k in range(4):
        send_a(k).start()

    eye = (lax.broadcasted_iota(jnp.int32, (NB, NB), 0) == lax.broadcasted_iota(jnp.int32, (NB, NB), 1)).astype(F32)

    def add_shift(side, l, cond):
        @pl.when(jnp.logical_and(p == 0, cond))
        def _():
            panel = 2 * l + side
            rs = row0(panel * NB, NB)
            w_buf[side, rs, l * NB:(l + 1) * NB] = w_buf[side, rs, l * NB:(l + 1) * NB] + eye * s_ref[pl.ds(panel, 1), :]

    acc1[...] = jnp.zeros_like(acc1)
    acc2[...] = jnp.zeros_like(acc2)
    ymax[...] = jnp.zeros_like(ymax)

    @pl.loop(0, n_l)
    def _(j):
        for cp in load(j):
            cp.wait()
        for l in range(2):
            add_shift(c, l, j == 0)
        rs = pl.ds(pl.multiple_of(j * ca, ca), ca)
        left = w_buf[c, rs, :]
        right = y_buf[rs, :]
        ymax[...] = jnp.maximum(ymax[...], jnp.max(jnp.abs(right).reshape(ca // 8, 8, half), axis=0))
        acc1[...] += dot_tn(left, jnp.concatenate([left, right], axis=1))

    def pair_copy(src, dst, slot, peer):
        return pltpu.make_async_remote_copy(src, dst, ar_send.at[slot], ar_recv.at[slot], device_id={'prow': peer}, device_id_type=MESH)

    g1 = pair_copy(acc1, acc1_r.at[0], 0, core_peer)
    g1.start()
    g1.wait()
    acc1[...] += acc1_r[0]
    g2 = pair_copy(acc1, acc1_r.at[1], 1, x_peer)
    g2.start()
    g2.wait()
    acc1[...] += acc1_r[1]
    h_buf[c] = acc1[:, :half]
    quarter = pl.ds(pl.multiple_of(p * qr, qr), qr)
    gy = pltpu.make_async_remote_copy(h_buf.at[c, quarter, :], h_buf.at[c, quarter, :], gy_send, gy_recv,
                                      device_id={'pcol': other}, device_id_type=MESH)
    gy.start()
    for k in range(4, n_a):
        send_a(k).start()
    send_b(0, 0).start()

    @pl.loop(0, n_a)
    def _(k):
        send_a(k).wait_recv()
        for l in range(2):
            add_shift(other, l, jnp.logical_and(c == 1, k == 0))
        rs = row0(other * half_rows + k * ca, ca)
        right = jnp.concatenate([w_buf[c, rs, :], y_buf[rs, :]], axis=1)
        acc2[...] += dot_tn(w_buf[other, rs, :], right)

        @pl.when(k == n_a - 2)
        def _():
            gy.wait()
            for d in range(1, 4):
                pltpu.make_async_remote_copy(h_buf.at[other, quarter, :], h_buf.at[other, quarter, :], gq_send.at[d], gq_recv.at[d],
                                             device_id={'prow': (p + d) % 4}, device_id_type=MESH).start()

    @pl.when(c == 0)
    def _():
        ct = acc2[:, :half].T
        for q in range(4):
            cm_buf[q, :qr, :] = ct[q * qr:(q + 1) * qr]

    @pl.when(c == 1)
    def _():
        for q in range(4):
            cm_buf[q, :qr, :] = acc2[q * qr:(q + 1) * qr, :half]

    for q in range(4):
        cm_buf[q, qr:, :] = ymax[...]

    def scatter(d):
        q = (p + d) % 4
        return pltpu.make_async_remote_copy(cm_buf.at[q], cm_recv.at[d - 1], rs_send.at[d], rs_recv.at[d],
                                            device_id={'prow': q}, device_id_type=MESH)

    for d in range(1, 4):
        scatter(d).start()
    for l in range(2):
        xp[l] = acc2[l * NB:(l + 1) * NB, half:]
    for d in range(1, 4):
        pltpu.make_async_remote_copy(h_buf.at[other, quarter, :], h_buf.at[other, quarter, :], gq_send.at[d], gq_recv.at[d],
                                     device_id={'prow': (p + d) % 4}, device_id_type=MESH).wait_send()
        src_q = pl.ds(pl.multiple_of(((p + 4 - d) % 4) * qr, qr), qr)
        pltpu.make_async_remote_copy(h_buf.at[other, src_q, :], h_buf.at[other, src_q, :], gq_send.at[d], gq_recv.at[d],
                                     device_id={'prow': (p + d) % 4}, device_id_type=MESH).wait_recv()
    for d in range(1, 4):
        scatter(d).wait()
    cm_buf[p] = ((cm_buf[p] + cm_recv[0]) + cm_recv[1]) + cm_recv[2]
    cy = pltpu.make_async_remote_copy(cm_buf.at[p], cy_recv, cy_send, cy_rsem, device_id={'pcol': other}, device_id_type=MESH)
    cy.start()
    for k in range(1, n_b):
        send_b(0, k).start()
    for k in range(n_b):
        send_b(1, k).start()
    cy.wait()
    cfin[p] = cm_buf[p] + cy_recv[...]

    def spread(d, src):
        return pltpu.make_async_remote_copy(cfin.at[src], cfin.at[src], ag_send.at[d], ag_recv.at[d],
                                            device_id={'prow': (p + d) % 4}, device_id_type=MESH)

    for d in range(1, 4):
        spread(d, p).start()

    factor_block(h_buf[0, :NB, :NB], u_blk, m_blk)

    for d in range(1, 4):
        spread(d, p).wait_send()
        spread(d, (p + 4 - d) % 4).wait_recv()

    cross = jnp.concatenate([cfin[q, :qr, :] for q in range(4)], axis=0)
    z_buf[...] = jnp.zeros_like(z_buf)
    diag_max = jnp.zeros((1, NB), F32)
    diag_min = jnp.full((1, NB), jnp.inf, F32)
    diags = []
    for i in range(4):
        ci, li = i % 2, i // 2
        for j in range(i, 4):
            cj, lj = j % 2, j // 2
            if ci == cj:
                block = h_buf[ci, li * NB:(li + 1) * NB, lj * NB:(lj + 1) * NB]
            elif ci == 0:
                block = cross[li * NB:(li + 1) * NB, lj * NB:(lj + 1) * NB]
            else:
                block = cross[lj * NB:(lj + 1) * NB, li * NB:(li + 1) * NB].T
            z_buf[i * NB:(i + 1) * NB, j * NB:(j + 1) * NB] = block
            if i == j:
                d_row = jnp.sum(block * eye, axis=0, keepdims=True)
                diags.append(d_row)
                diag_max = jnp.maximum(diag_max, d_row)
                diag_min = jnp.minimum(diag_min, d_row)

    t_buf[...] = jnp.zeros_like(t_buf)
    rf_buf[...] = jnp.zeros_like(rf_buf)
    for j in range(4):
        lo, hi = j * NB, (j + 1) * NB
        if j > 0:
            factor_block(z_buf[lo:hi, lo:hi], u_blk, m_blk)
        inv_t = m_blk[...]
        rf_buf[lo:hi, lo:hi] = u_blk[...]
        t_buf[lo:hi, lo:hi] = inv_t
        new_row = dot_nn(inv_t, z_buf[lo:hi, :])
        if j > 0:
            t_buf[lo:hi, :lo] = new_row[:, :lo]
        if j < 3:
            rf_buf[lo:hi, hi:] = new_row[:, hi:]
            parts = ([new_row[:, :lo]] if j > 0 else []) + [inv_t, new_row[:, hi:]]
            mult = jnp.concatenate(parts, axis=1)
            z_buf[hi:, lo:hi] = jnp.zeros((kk - hi, NB), F32)
            z_buf[hi:, :] = z_buf[hi:, :] - dot_tn(new_row[:, hi:], mult)

    trace = jnp.zeros((1, NB), F32)
    for i in range(4):
        tc = t_buf[i * NB:, i * NB:(i + 1) * NB]
        trace = trace + jnp.sum(tc * tc, axis=0, keepdims=True) * diags[i]
    total = jnp.sum(trace, axis=1, keepdims=True)
    d_max = jnp.max(diag_max, axis=1, keepdims=True)
    d_min = jnp.min(diag_min, axis=1, keepdims=True)
    y_max = jnp.max(jnp.max(cfin[0, qr:, :], axis=0, keepdims=True), axis=1, keepdims=True)
    good = (total < TRACE_FACTOR * kk) & (d_min > 1e-26) & (d_max < 1e36) & (y_max * jnp.sqrt(d_max) < 1e33)
    ok_ref[...] = jnp.broadcast_to(jnp.where(good, 1.0, 0.0), ok_ref.shape)

    for l in range(2):
        ls = pl.ds(pl.multiple_of((2 * l + c) * NB, NB), NB)
        r_buf[:, l * NB:(l + 1) * NB] = rf_buf[:, ls]

    k12[row0(c * NB, NB), :] = acc1[:NB, half:]
    k12[row0((c + 2) * NB, NB), :] = acc1[NB:, half:]
    k12[row0((3 - c) * NB, NB), :] = jnp.zeros((NB, half), F32)

    def take_b(l, k):
        send_b(l, k).wait_recv()
        if k == 0:
            add_shift(other, l, c == 0)
        rs = row0(c * half_rows + k * cb, cb)
        xp[l] += dot_tn(w_buf[other, rs, l * NB:(l + 1) * NB], y_buf[rs, :])

    for k in range(n_b):
        take_b(0, k)
    x1 = pair_copy(xp.at[0], xp_r.at[0], 2, core_peer)
    x1.start()
    x1.wait()
    xp[0] = xp[0] + xp_r[0]
    x2 = pair_copy(xp.at[0], xp_r.at[1], 3, x_peer)
    x2.start()
    take_b(1, 0)
    x2.wait()
    k12[row0((1 - c) * NB, NB), :] = xp[0] + xp_r[1]
    r_buf[:, half:] = dot_nn(t_buf[...], k12[...])
    for k in range(1, n_b):
        take_b(1, k)
    x3 = pair_copy(xp.at[1], xp_r.at[2], 4, core_peer)
    x3.start()
    x3.wait()
    xp[1] = xp[1] + xp_r[2]
    x4 = pair_copy(xp.at[1], xp_r.at[3], 5, x_peer)
    x4.start()
    x4.wait()
    last = xp[1] + xp_r[3]
    r_buf[half:, half:] += dot_nn(t_buf[half:, pl.ds(pl.multiple_of((3 - c) * NB, NB), NB)], last)
    out = pltpu.make_async_copy(r_buf, r_hbm, out_sem)
    out.start()

    for k in range(n_a):
        send_a(k).wait_send()
    for l in range(2):
        for k in range(n_b):
            send_b(l, k).wait_send()
    out.wait()


def gram_rows(a_loc, diag_shift):
    rows, cols = a_loc.shape
    half = cols // 2
    kk = cols
    qr = half // 4
    dma = pltpu.SemaphoreType.DMA
    vm = lambda *shape: pltpu.VMEM(shape, F32)
    return pl.pallas_call(
        gram_kernel,
        out_shape=(jax.ShapeDtypeStruct((kk, cols), F32), jax.ShapeDtypeStruct((8, NB), F32)),
        in_specs=[pl.BlockSpec(memory_space=pl.ANY), pl.BlockSpec(memory_space=pltpu.VMEM)],
        out_specs=(pl.BlockSpec(memory_space=pl.ANY), pl.BlockSpec(memory_space=pltpu.VMEM)),
        scratch_shapes=[
            vm(2, rows, half), vm(rows, half), vm(half, cols), vm(half, cols), vm(2, half, cols), vm(2, half, half),
            vm(4, qr + 8, half), vm(3, qr + 8, half), vm(qr + 8, half), vm(4, qr + 8, half),
            vm(2, NB, half), vm(4, NB, half), vm(kk, kk), vm(kk, kk), vm(kk, kk), vm(kk, half), vm(kk, cols), vm(8, half),
            vm(NB, NB), vm(NB, NB),
            dma((2, rows // 512)), dma((rows // 1024,)), dma((rows // 1024,)), dma((2, rows // 1536)), dma((2, rows // 1536)),
            dma((6,)), dma((6,)), dma, dma, dma((4,)), dma((4,)),
            dma((4,)), dma((4,)), dma, dma, dma((4,)), dma((4,)), dma,
        ],
        compiler_params=pltpu.CompilerParams(collective_id=0, has_side_effects=True, vmem_limit_bytes=56 * 1024 * 1024),
        name='gram_rows',
    )(a_loc, diag_shift)


def solution(mesh):
    n_pcol = mesh.shape['pcol']

    def local_qr(a_loc, diag_shift):
        rows, ok = gram_rows(a_loc, diag_shift)
        return lax.cond(ok[0, 0] > 0.5, lambda a, s, r: r, lambda a, s, r: householder_rows(a, s, n_pcol), a_loc, diag_shift, rows)

    return jax.shard_map(local_qr, mesh=mesh, in_specs=(P(('batch', 'prow'), 'pcol'), P('batch', None)), out_specs=P('batch', 'pcol'), check_vma=False)
```

time: 11000 us -> 168 us (0.02); the launches traced: 10900 us -> 168 us
  blocking collectives: 3060 us -> 0 us
  matrix products: 2200 us -> 0 us
  local copies, waits for them, and re-layouts: 2190 us -> 3.46 us
  loops' own time: 2060 us -> 0.01 us
  other arithmetic: 870 us -> 0 us
  waiting for transfers between devices: 471 us -> 0 us
  Pallas kernels: 0 us -> 163 us
    psum x513 -> x0, blocking collectives: 3060 us -> none  [the longest x512 3060 us: col_step(): lax.psum(jnp.dot(stacked, panel, precision=PRECISE, preferred_element_typ...]
    dot_general x1040 -> x0, matrix products: 2200 us -> none  [the longest x512 1290 us: col_step(): jnp.dot(stacked, panel, precision=PRECISE, preferred_element_type=jnp.flo...]
    another operation x8 -> x1, loops' own time: 2060 us -> 0.01 us  [local_qr(): lax.cond(ok[0, 0] > 0.5, lambda a, s, r: r, lambda a, s, r: householder_r...]
    dynamic_update_slice x1024 -> x0, local copies, waits for them, and re-layouts: 1170 us -> none  [the longest x512 870 us: col_step(): lax.dynamic_update_slice_in_dim(vectors, v_col[:, None], k, axis=1)]
    dynamic_slice x1024 -> x0, local copies, waits for them, and re-layouts: 610 us -> none  [the longest x512 308 us: col_step(): pivot_val = lax.dynamic_index_in_dim(pivot_row, k, keepdims=False)]
    psum x13 -> x0, waiting for transfers between devices: 471 us -> none  [the longest x8 341 us: local_qr(): lax.psum((jnp.where(is_owner, vectors, 0.0), jnp.where(is_owner, t_factor...]
    mul x513 -> x0, other arithmetic: 341 us -> none  [the longest x512 339 us: col_step(): panel = panel - v_col[:, None] * update[None, :]]
    sub x512 -> x0, other arithmetic: 338 us -> none  [col_step(): panel = panel - v_col[:, None] * update[None, :]]
where the time goes in v1:
time: 168 us
  Pallas kernels  163 us (97%)
  local copies, waits for them, and re-layouts  3.46 us (2%)
    pallas_call x1, Pallas kernels, gram_rows(): pl.pallas_call(gram_kernel, out_shape=(jax.ShapeDtypeStruct((kk, cols), F...  163 us

profile of v1, /device:TPU:0, one launch (start us, length us, event | category | flops | bytes accessed | tf_op | source)
XLA Modules:
  0.0 167.6 jit_solution(15768496407597642137)
XLA Ops:
  0.0 0.0 copy-start
  0.0 163.4 %gram_rows.1 = (f32[512,512]{1,0:T(8,128)}, f32[8,128]{1,0:T(8,128)}) custom-call(f32[6144,512]{1,0:T(8,128)} %a_hbm.1, f32[4,128]{1,0:T(4,128)} %s_ref.1), custom_call_target="tpu_custom_call" | custom-call | tf_op jit(solution)/shard_map/gram_rows/pallas_call | solution.py:434
  163.4 1.2 slice.64
  165.3 0.0 copy-done
  165.3 2.3 %copy.66 = f32[512,512]{1,0:T(8,128)} copy(f32[512,512]{1,0:T(8,128)} %get-tuple-element.517) | data formatting | bytes 2097152
  (1 shorter events, 0.0 us)
Async XLA Ops:
  0.0 165.3 %copy-start = (f32[4,128]{1,0:T(4,128)S(1)}, f32[4,128]{1,0:T(4,128)}, u32[]{:S(2)}) copy-start(f32[4,128]{1,0:T(4,128)} %s_ref.1) | copy-start | bytes 6148

commit v2 on v1

--- a/solution.py
+++ b/solution.py
@@ -127,39 +127,62 @@
     sub = lax.broadcasted_iota(jnp.int32, (8, NB), 0)
     lane = lax.broadcasted_iota(jnp.int32, (8, NB), 1)
     eye = (lax.broadcasted_iota(jnp.int32, (NB, NB), 0) == lax.broadcasted_iota(jnp.int32, (NB, NB), 1)).astype(F32)
-
-    def group(g, state):
-        s_mat, m_mat = state
-        for t in range(8):
-            row_s = s_mat[t:t + 1, :]
-            row_m = m_mat[t:t + 1, :]
-            inv_p = 1.0 / s_mat[t:t + 1, t:t + 1]
-            row_s = row_s * inv_p
-            row_m = row_m * inv_p
-            col = s_mat[:, t:t + 1]
-            top = jnp.where(sub[:, 0:1] > t, col[:8], 0.0)
-            col = jnp.concatenate([top, col[8:]], axis=0)
-            s_mat = s_mat - col * row_s
-            m_mat = m_mat - col * row_m
-        s_top, m_top = s_mat[:8], m_mat[:8]
-        diag = jnp.sum(jnp.where(lane == sub, s_top, 0.0), axis=1, keepdims=True)
-        scale = 1.0 / jnp.sqrt(diag)
+    wide = lambda row: jnp.broadcast_to(row, (8, NB))
+
+    def group(tiles, g, state):
+        s_tiles, m_tiles = state[:tiles], state[tiles:]
         base = pl.multiple_of(g * 8, 8)
-        u_top = pltpu.roll(jnp.where(lane >= sub, s_top * scale, 0.0), base, 1)
-        u_ref[pl.ds(base, 8), :] = jnp.where(lane >= sub + base, u_top, 0.0)
+        spread = lambda tile, t: jnp.take_along_axis(tile, jnp.full((8, NB), base + t, jnp.int32), axis=1)
+        s_top, m_top = s_tiles[0], m_tiles[0]
+        cols = [spread(s_top, t) for t in range(8)]
+        dinv = jnp.zeros((8, NB), F32)
+        for s in range(8):
+            inv_p = 1.0 / wide(cols[s][s:s + 1])
+            dinv = jnp.where(sub == s, inv_p, dinv)
+            mult = jnp.where(sub > s, cols[s] * inv_p, 0.0)
+            for t in range(s + 1, 8):
+                cols[t] = cols[t] - mult * wide(cols[t][s:s + 1])
+            s_top = s_top - mult * wide(s_top[s:s + 1])
+            m_top = m_top - mult * wide(m_top[s:s + 1])
+        scale = jnp.sqrt(dinv)
+        u_ref[pl.ds(base, 8), :] = jnp.where(lane >= sub + base, s_top * scale, 0.0)
         m_ref[pl.ds(base, 8), :] = m_top * scale
+        s_sol, m_sol = s_top * dinv, m_top * dinv
+        for s in range(7, 0, -1):
+            mult = jnp.where(sub < s, cols[s] * dinv, 0.0)
+            s_sol = s_sol - mult * wide(s_sol[s:s + 1])
+            m_sol = m_sol - mult * wide(m_sol[s:s + 1])
+        s_rows = [wide(s_sol[t:t + 1]) for t in range(8)]
+        m_rows = [wide(m_sol[t:t + 1]) for t in range(8)]
+        s_new, m_new = [], []
+        for v in range(1, tiles):
+            s_acc, m_acc = s_tiles[v], m_tiles[v]
+            for t in range(8):
+                col = spread(s_tiles[v], t)
+                s_acc = s_acc - col * s_rows[t]
+                m_acc = m_acc - col * m_rows[t]
+            s_new.append(s_acc)
+            m_new.append(m_acc)
         zero = jnp.zeros((8, NB), F32)
-        s_mat = pltpu.roll(jnp.concatenate([s_mat[8:], zero], axis=0), NB - 8, 1)
-        m_mat = jnp.concatenate([m_mat[8:], zero], axis=0)
-        return s_mat, m_mat
-
-    lax.fori_loop(0, NB // 8, group, (block, eye))
-
-
-def gram_kernel(a_hbm, s_ref, r_hbm, ok_ref, w_buf, y_buf, acc1, acc2, acc1_r, h_buf, cm_buf, cm_recv, cy_recv, cfin,
-                xp, xp_r, z_buf, t_buf, rf_buf, k12, r_buf, ymax, u_blk, m_blk,
+        return tuple(s_new + [zero] + m_new + [zero])
+
+    def tiles_of(x):
+        return [x[8 * v:8 * v + 8] for v in range(x.shape[0] // 8)]
+
+    n = NB // 8
+    state = tuple(tiles_of(block) + tiles_of(eye))
+    done = 0
+    for tiles, steps in ((n, n // 2), (n // 2, n // 2)):
+        state = lax.fori_loop(done, done + steps, functools.partial(group, tiles), state)
+        done += steps
+        half = len(state) // 2
+        state = state[:n - done] + state[half:half + n - done]
+
+
+def gram_kernel(a_hbm, s_hbm, r_hbm, ok_hbm, s_ref, ok_ref, w_buf, y_buf, acc1, acc2, acc1_r, h_buf, cm_buf, cm_recv, cy_recv, cfin,
+                xp, xp_r, tail_r, tail_s, last_buf, z_buf, t_buf, rf_buf, k12, r_buf, ymax, u_blk, m_blk,
                 load_sem, ya_send, ya_recv, yb_send, yb_recv, ar_send, ar_recv, gy_send, gy_recv, gq_send, gq_recv,
-                rs_send, rs_recv, cy_send, cy_rsem, ag_send, ag_recv, out_sem):
+                rs_send, rs_recv, cy_send, cy_rsem, ag_send, ag_recv, s_sem, out_sem):
     rows, cols = a_hbm.shape
     half_rows = rows // 2
     half = cols // 2
@@ -172,8 +195,8 @@
     qr = half // 4
     ca = 512
     n_a = half_rows // ca
-    cb = 768
-    n_b = half_rows // cb
+    b_cuts = ((0, 768, 1920, 3072), (0, 1024, 2048, 2816, 3072))
+    n_b = [len(cuts) - 1 for cuts in b_cuts]
     n_l = rows // ca
 
     def row0(start, size):
@@ -184,14 +207,15 @@
         return (pltpu.make_async_copy(a_hbm.at[rs, pl.ds(0, half)], w_buf.at[c, rs, :], load_sem.at[0, j]),
                 pltpu.make_async_copy(a_hbm.at[rs, pl.ds(half, half)], y_buf.at[rs, :], load_sem.at[1, j]))
 
-    for j in range(n_l):
-        for cp in load(j):
-            cp.start()
-
     barrier = pltpu.get_barrier_semaphore()
     pl.semaphore_signal(barrier, inc=1, device_id={'pcol': other}, device_id_type=MESH)
     for d in range(1, 4):
         pl.semaphore_signal(barrier, inc=1, device_id={'prow': (p + d) % 4}, device_id_type=MESH)
+    s_load = pltpu.make_async_copy(s_hbm, s_ref, s_sem)
+    s_load.start()
+    for j in range(n_l):
+        for cp in load(j):
+            cp.start()
     pl.semaphore_wait(barrier, 4)
 
     def send_a(k):
@@ -200,7 +224,7 @@
                                             device_id={'pcol': other}, device_id_type=MESH)
 
     def send_b(l, k):
-        rs = row0(other * half_rows + k * cb, cb)
+        rs = row0(other * half_rows + b_cuts[l][k], b_cuts[l][k + 1] - b_cuts[l][k])
         ls = pl.ds(l * NB, NB)
         return pltpu.make_async_remote_copy(a_hbm.at[rs, ls], w_buf.at[c, rs, ls], yb_send.at[l, k], yb_recv.at[l, k],
                                             device_id={'pcol': other}, device_id_type=MESH)
@@ -220,6 +244,7 @@
     acc1[...] = jnp.zeros_like(acc1)
     acc2[...] = jnp.zeros_like(acc2)
     ymax[...] = jnp.zeros_like(ymax)
+    s_load.wait()
 
     @pl.loop(0, n_l)
     def _(j):
@@ -253,8 +278,7 @@
         send_a(k).start()
     send_b(0, 0).start()
 
-    @pl.loop(0, n_a)
-    def _(k):
+    def take_a(k):
         send_a(k).wait_recv()
         for l in range(2):
             add_shift(other, l, jnp.logical_and(c == 1, k == 0))
@@ -262,12 +286,27 @@
         right = jnp.concatenate([w_buf[c, rs, :], y_buf[rs, :]], axis=1)
         acc2[...] += dot_tn(w_buf[other, rs, :], right)
 
-        @pl.when(k == n_a - 2)
+    def spread_gram(d, src):
+        rs = pl.ds(pl.multiple_of(src * qr, qr), qr)
+        return pltpu.make_async_remote_copy(h_buf.at[other, rs, :], h_buf.at[other, rs, :], gq_send.at[d], gq_recv.at[d],
+                                            device_id={'prow': (p + d) % 4}, device_id_type=MESH)
+
+    @pl.loop(0, n_a)
+    def _(k):
+        take_a(k)
+
+        @pl.when(k == n_a - 3)
         def _():
             gy.wait()
             for d in range(1, 4):
-                pltpu.make_async_remote_copy(h_buf.at[other, quarter, :], h_buf.at[other, quarter, :], gq_send.at[d], gq_recv.at[d],
-                                             device_id={'prow': (p + d) % 4}, device_id_type=MESH).start()
+                spread_gram(d, p).start()
+
+        @pl.when(k == n_a - 2)
+        def _():
+            for d in range(1, 4):
+                spread_gram(d, p).wait_send()
+                spread_gram(d, (p + 4 - d) % 4).wait_recv()
+            factor_block(h_buf[0, :NB, :NB], u_blk, m_blk)
 
     @pl.when(c == 0)
     def _():
@@ -293,19 +332,13 @@
     for l in range(2):
         xp[l] = acc2[l * NB:(l + 1) * NB, half:]
     for d in range(1, 4):
-        pltpu.make_async_remote_copy(h_buf.at[other, quarter, :], h_buf.at[other, quarter, :], gq_send.at[d], gq_recv.at[d],
-                                     device_id={'prow': (p + d) % 4}, device_id_type=MESH).wait_send()
-        src_q = pl.ds(pl.multiple_of(((p + 4 - d) % 4) * qr, qr), qr)
-        pltpu.make_async_remote_copy(h_buf.at[other, src_q, :], h_buf.at[other, src_q, :], gq_send.at[d], gq_recv.at[d],
-                                     device_id={'prow': (p + d) % 4}, device_id_type=MESH).wait_recv()
-    for d in range(1, 4):
         scatter(d).wait()
     cm_buf[p] = ((cm_buf[p] + cm_recv[0]) + cm_recv[1]) + cm_recv[2]
     cy = pltpu.make_async_remote_copy(cm_buf.at[p], cy_recv, cy_send, cy_rsem, device_id={'pcol': other}, device_id_type=MESH)
     cy.start()
-    for k in range(1, n_b):
+    for k in range(1, n_b[0]):
         send_b(0, k).start()
-    for k in range(n_b):
+    for k in range(n_b[1]):
         send_b(1, k).start()
     cy.wait()
     cfin[p] = cm_buf[p] + cy_recv[...]
@@ -316,8 +349,6 @@
 
     for d in range(1, 4):
         spread(d, p).start()
-
-    factor_block(h_buf[0, :NB, :NB], u_blk, m_blk)
 
     for d in range(1, 4):
         spread(d, p).wait_send()
@@ -374,10 +405,19 @@
     y_max = jnp.max(jnp.max(cfin[0, qr:, :], axis=0, keepdims=True), axis=1, keepdims=True)
     good = (total < TRACE_FACTOR * kk) & (d_min > 1e-26) & (d_max < 1e36) & (y_max * jnp.sqrt(d_max) < 1e33)
     ok_ref[...] = jnp.broadcast_to(jnp.where(good, 1.0, 0.0), ok_ref.shape)
+    ok_out = pltpu.make_async_copy(ok_ref, ok_hbm, out_sem.at[0])
+    ok_out.start()
 
     for l in range(2):
         ls = pl.ds(pl.multiple_of((2 * l + c) * NB, NB), NB)
         r_buf[:, l * NB:(l + 1) * NB] = rf_buf[:, ls]
+
+    def out_copy(i, rows_i, cols_i):
+        return pltpu.make_async_copy(r_buf.at[rows_i, cols_i], r_hbm.at[rows_i, cols_i], out_sem.at[i])
+
+    outs = [out_copy(1, pl.ds(0, kk), pl.ds(0, half)), out_copy(2, pl.ds(0, half), pl.ds(half, half)),
+            out_copy(3, pl.ds(half, half), pl.ds(half, half))]
+    outs[0].start()
 
     k12[row0(c * NB, NB), :] = acc1[:NB, half:]
     k12[row0((c + 2) * NB, NB), :] = acc1[NB:, half:]
@@ -387,10 +427,10 @@
         send_b(l, k).wait_recv()
         if k == 0:
             add_shift(other, l, c == 0)
-        rs = row0(c * half_rows + k * cb, cb)
+        rs = row0(c * half_rows + b_cuts[l][k], b_cuts[l][k + 1] - b_cuts[l][k])
         xp[l] += dot_tn(w_buf[other, rs, l * NB:(l + 1) * NB], y_buf[rs, :])
 
-    for k in range(n_b):
+    for k in range(n_b[0]):
         take_b(0, k)
     x1 = pair_copy(xp.at[0], xp_r.at[0], 2, core_peer)
     x1.start()
@@ -398,30 +438,36 @@
     xp[0] = xp[0] + xp_r[0]
     x2 = pair_copy(xp.at[0], xp_r.at[1], 3, x_peer)
     x2.start()
-    take_b(1, 0)
     x2.wait()
     k12[row0((1 - c) * NB, NB), :] = xp[0] + xp_r[1]
     r_buf[:, half:] = dot_nn(t_buf[...], k12[...])
-    for k in range(1, n_b):
+    outs[1].start()
+    for k in range(n_b[1]):
         take_b(1, k)
-    x3 = pair_copy(xp.at[1], xp_r.at[2], 4, core_peer)
+    mine = pl.ds(pl.multiple_of((p % 2) * (NB // 2), NB // 2), NB // 2)
+    theirs = pl.ds(pl.multiple_of((1 - p % 2) * (NB // 2), NB // 2), NB // 2)
+    x3 = pair_copy(xp.at[1, theirs, :], tail_r.at[0], 4, core_peer)
     x3.start()
     x3.wait()
-    xp[1] = xp[1] + xp_r[2]
-    x4 = pair_copy(xp.at[1], xp_r.at[3], 5, x_peer)
+    tail_s[...] = xp[1, mine, :] + tail_r[0]
+    x4 = pair_copy(tail_s, tail_r.at[1], 5, x_peer)
     x4.start()
     x4.wait()
-    last = xp[1] + xp_r[3]
-    r_buf[half:, half:] += dot_nn(t_buf[half:, pl.ds(pl.multiple_of((3 - c) * NB, NB), NB)], last)
-    out = pltpu.make_async_copy(r_buf, r_hbm, out_sem)
-    out.start()
+    last_buf[mine, :] = tail_s[...] + tail_r[1]
+    x5 = pair_copy(last_buf.at[mine, :], last_buf.at[mine, :], 6, core_peer)
+    x5.start()
+    x5.wait()
+    r_buf[half:, half:] += dot_nn(t_buf[half:, pl.ds(pl.multiple_of((3 - c) * NB, NB), NB)], last_buf[...])
+    outs[2].start()
 
     for k in range(n_a):
         send_a(k).wait_send()
     for l in range(2):
-        for k in range(n_b):
+        for k in range(n_b[l]):
             send_b(l, k).wait_send()
-    out.wait()
+    ok_out.wait()
+    for out in outs:
+        out.wait()
 
 
 def gram_rows(a_loc, diag_shift):
@@ -434,16 +480,17 @@
     return pl.pallas_call(
         gram_kernel,
         out_shape=(jax.ShapeDtypeStruct((kk, cols), F32), jax.ShapeDtypeStruct((8, NB), F32)),
-        in_specs=[pl.BlockSpec(memory_space=pl.ANY), pl.BlockSpec(memory_space=pltpu.VMEM)],
-        out_specs=(pl.BlockSpec(memory_space=pl.ANY), pl.BlockSpec(memory_space=pltpu.VMEM)),
+        in_specs=[pl.BlockSpec(memory_space=pl.ANY), pl.BlockSpec(memory_space=pl.ANY)],
+        out_specs=(pl.BlockSpec(memory_space=pl.ANY), pl.BlockSpec(memory_space=pl.ANY)),
         scratch_shapes=[
+            vm(*diag_shift.shape), vm(8, NB),
             vm(2, rows, half), vm(rows, half), vm(half, cols), vm(half, cols), vm(2, half, cols), vm(2, half, half),
             vm(4, qr + 8, half), vm(3, qr + 8, half), vm(qr + 8, half), vm(4, qr + 8, half),
-            vm(2, NB, half), vm(4, NB, half), vm(kk, kk), vm(kk, kk), vm(kk, kk), vm(kk, half), vm(kk, cols), vm(8, half),
+            vm(2, NB, half), vm(2, NB, half), vm(2, NB // 2, half), vm(NB // 2, half), vm(NB, half), vm(kk, kk), vm(kk, kk), vm(kk, kk), vm(kk, half), vm(kk, cols), vm(8, half),
             vm(NB, NB), vm(NB, NB),
-            dma((2, rows // 512)), dma((rows // 1024,)), dma((rows // 1024,)), dma((2, rows // 1536)), dma((2, rows // 1536)),
-            dma((6,)), dma((6,)), dma, dma, dma((4,)), dma((4,)),
-            dma((4,)), dma((4,)), dma, dma, dma((4,)), dma((4,)), dma,
+            dma((2, rows // 512)), dma((rows // 1024,)), dma((rows // 1024,)), dma((2, 4)), dma((2, 4)),
+            dma((7,)), dma((7,)), dma, dma, dma((4,)), dma((4,)),
+            dma((4,)), dma((4,)), dma, dma, dma((4,)), dma((4,)), dma, dma((4,)),
         ],
         compiler_params=pltpu.CompilerParams(collective_id=0, has_side_effects=True, vmem_limit_bytes=56 * 1024 * 1024),
         name='gram_rows',

time: 168 us -> 155 us (0.923)
  Pallas kernels: 163 us -> 151 us
    pallas_call x1, Pallas kernels: 163 us -> 151 us  [gram_rows(): pl.pallas_call(gram_kernel, out_shape=(jax.ShapeDtypeStruct((kk, cols), F...]
where the time goes in v2:
time: 155 us
  Pallas kernels  151 us (97%)
  local copies, waits for them, and re-layouts  3.46 us (2%)
    pallas_call x1, Pallas kernels, gram_rows(): pl.pallas_call(gram_kernel, out_shape=(jax.ShapeDtypeStruct((kk, cols), F...  151 us

profile of v2, /device:TPU:0, one launch (start us, length us, event | category | flops | bytes accessed | tf_op | source)
XLA Modules:
  0.0 155.3 jit_solution(3366626750794770052)
XLA Ops:
  0.0 0.0 copy-start
  0.0 151.2 %gram_rows.1 = (f32[512,512]{1,0:T(8,128)}, f32[8,128]{1,0:T(8,128)}) custom-call(f32[6144,512]{1,0:T(8,128)} %a_hbm.1, f32[4,128]{1,0:T(4,128)} %s_hbm.1), custom_call_target="tpu_custom_call" | custom-call | tf_op jit(solution)/shard_map/gram_rows/pallas_call | solution.py:480
  151.2 1.2 slice.64
  153.0 0.0 copy-done
  153.0 2.3 %copy.66 = f32[512,512]{1,0:T(8,128)} copy(f32[512,512]{1,0:T(8,128)} %get-tuple-element.517) | data formatting | bytes 2097152
  (1 shorter events, 0.0 us)
Async XLA Ops:
  0.0 153.0 %copy-start = (f32[4,128]{1,0:T(4,128)S(1)}, f32[4,128]{1,0:T(4,128)}, u32[]{:S(2)}) copy-start(f32[4,128]{1,0:T(4,128)} %s_hbm.1) | copy-start | bytes 6148

commit v3 on v2

--- a/solution.py
+++ b/solution.py
@@ -179,10 +179,10 @@
         state = state[:n - done] + state[half:half + n - done]
 
 
-def gram_kernel(a_hbm, s_hbm, r_hbm, ok_hbm, s_ref, ok_ref, w_buf, y_buf, acc1, acc2, acc1_r, h_buf, cm_buf, cm_recv, cy_recv, cfin,
-                xp, xp_r, tail_r, tail_s, last_buf, z_buf, t_buf, rf_buf, k12, r_buf, ymax, u_blk, m_blk,
+def gram_kernel(a_hbm, s_hbm, r_ref, ok_ref, s_ref, w_buf, y_buf, acc1, acc2, acc1_r, h_buf, cm_buf, cm_recv, cy_recv, cfin,
+                xp, xp_r, tail_r, tail_s, last_buf, z_buf, t_buf, rf_buf, k12, ymax, u_blk, m_blk,
                 load_sem, ya_send, ya_recv, yb_send, yb_recv, ar_send, ar_recv, gy_send, gy_recv, gq_send, gq_recv,
-                rs_send, rs_recv, cy_send, cy_rsem, ag_send, ag_recv, s_sem, out_sem):
+                rs_send, rs_recv, cy_send, cy_rsem, ag_send, ag_recv, s_sem):
     rows, cols = a_hbm.shape
     half_rows = rows // 2
     half = cols // 2
@@ -404,20 +404,11 @@
     d_min = jnp.min(diag_min, axis=1, keepdims=True)
     y_max = jnp.max(jnp.max(cfin[0, qr:, :], axis=0, keepdims=True), axis=1, keepdims=True)
     good = (total < TRACE_FACTOR * kk) & (d_min > 1e-26) & (d_max < 1e36) & (y_max * jnp.sqrt(d_max) < 1e33)
-    ok_ref[...] = jnp.broadcast_to(jnp.where(good, 1.0, 0.0), ok_ref.shape)
-    ok_out = pltpu.make_async_copy(ok_ref, ok_hbm, out_sem.at[0])
-    ok_out.start()
+    ok_ref[0, 0] = jnp.where(good, 1, 0)[0, 0]
 
     for l in range(2):
         ls = pl.ds(pl.multiple_of((2 * l + c) * NB, NB), NB)
-        r_buf[:, l * NB:(l + 1) * NB] = rf_buf[:, ls]
-
-    def out_copy(i, rows_i, cols_i):
-        return pltpu.make_async_copy(r_buf.at[rows_i, cols_i], r_hbm.at[rows_i, cols_i], out_sem.at[i])
-
-    outs = [out_copy(1, pl.ds(0, kk), pl.ds(0, half)), out_copy(2, pl.ds(0, half), pl.ds(half, half)),
-            out_copy(3, pl.ds(half, half), pl.ds(half, half))]
-    outs[0].start()
+        r_ref[:, l * NB:(l + 1) * NB] = rf_buf[:, ls]
 
     k12[row0(c * NB, NB), :] = acc1[:NB, half:]
     k12[row0((c + 2) * NB, NB), :] = acc1[NB:, half:]
@@ -440,8 +431,7 @@
     x2.start()
     x2.wait()
     k12[row0((1 - c) * NB, NB), :] = xp[0] + xp_r[1]
-    r_buf[:, half:] = dot_nn(t_buf[...], k12[...])
-    outs[1].start()
+    r_ref[:, half:] = dot_nn(t_buf[...], k12[...])
     for k in range(n_b[1]):
         take_b(1, k)
     mine = pl.ds(pl.multiple_of((p % 2) * (NB // 2), NB // 2), NB // 2)
@@ -457,17 +447,13 @@
     x5 = pair_copy(last_buf.at[mine, :], last_buf.at[mine, :], 6, core_peer)
     x5.start()
     x5.wait()
-    r_buf[half:, half:] += dot_nn(t_buf[half:, pl.ds(pl.multiple_of((3 - c) * NB, NB), NB)], last_buf[...])
-    outs[2].start()
+    r_ref[half:, half:] += dot_nn(t_buf[half:, pl.ds(pl.multiple_of((3 - c) * NB, NB), NB)], last_buf[...])
 
     for k in range(n_a):
         send_a(k).wait_send()
     for l in range(2):
         for k in range(n_b[l]):
             send_b(l, k).wait_send()
-    ok_out.wait()
-    for out in outs:
-        out.wait()
 
 
 def gram_rows(a_loc, diag_shift):
@@ -479,20 +465,20 @@
     vm = lambda *shape: pltpu.VMEM(shape, F32)
     return pl.pallas_call(
         gram_kernel,
-        out_shape=(jax.ShapeDtypeStruct((kk, cols), F32), jax.ShapeDtypeStruct((8, NB), F32)),
+        out_shape=(pltpu.VMEM((kk, cols), F32), pltpu.SMEM((1, 1), jnp.int32)),
         in_specs=[pl.BlockSpec(memory_space=pl.ANY), pl.BlockSpec(memory_space=pl.ANY)],
-        out_specs=(pl.BlockSpec(memory_space=pl.ANY), pl.BlockSpec(memory_space=pl.ANY)),
+        out_specs=(pl.BlockSpec(memory_space=pltpu.VMEM), pl.BlockSpec(memory_space=pltpu.SMEM)),
         scratch_shapes=[
-            vm(*diag_shift.shape), vm(8, NB),
+            vm(*diag_shift.shape),
             vm(2, rows, half), vm(rows, half), vm(half, cols), vm(half, cols), vm(2, half, cols), vm(2, half, half),
             vm(4, qr + 8, half), vm(3, qr + 8, half), vm(qr + 8, half), vm(4, qr + 8, half),
-            vm(2, NB, half), vm(2, NB, half), vm(2, NB // 2, half), vm(NB // 2, half), vm(NB, half), vm(kk, kk), vm(kk, kk), vm(kk, kk), vm(kk, half), vm(kk, cols), vm(8, half),
+            vm(2, NB, half), vm(2, NB, half), vm(2, NB // 2, half), vm(NB // 2, half), vm(NB, half), vm(kk, kk), vm(kk, kk), vm(kk, kk), vm(kk, half), vm(8, half),
             vm(NB, NB), vm(NB, NB),
             dma((2, rows // 512)), dma((rows // 1024,)), dma((rows // 1024,)), dma((2, 4)), dma((2, 4)),
             dma((7,)), dma((7,)), dma, dma, dma((4,)), dma((4,)),
-            dma((4,)), dma((4,)), dma, dma, dma((4,)), dma((4,)), dma, dma((4,)),
+            dma((4,)), dma((4,)), dma, dma, dma((4,)), dma((4,)), dma,
         ],
-        compiler_params=pltpu.CompilerParams(collective_id=0, has_side_effects=True, vmem_limit_bytes=56 * 1024 * 1024),
+        compiler_params=pltpu.CompilerParams(collective_id=0, has_side_effects=True, vmem_limit_bytes=48 * 1024 * 1024),
         name='gram_rows',
     )(a_loc, diag_shift)
 
@@ -502,6 +488,6 @@
 
     def local_qr(a_loc, diag_shift):
         rows, ok = gram_rows(a_loc, diag_shift)
-        return lax.cond(ok[0, 0] > 0.5, lambda a, s, r: r, lambda a, s, r: householder_rows(a, s, n_pcol), a_loc, diag_shift, rows)
+        return lax.cond(ok[0, 0] != 0, lambda a, s, r: r, lambda a, s, r: householder_rows(a, s, n_pcol), a_loc, diag_shift, rows)
 
     return jax.shard_map(local_qr, mesh=mesh, in_specs=(P(('batch', 'prow'), 'pcol'), P('batch', None)), out_specs=P('batch', 'pcol'), check_vma=False)

time: 155 us -> 152 us (0.981)
  local copies, waits for them, and re-layouts: 3.46 us -> 0.98 us
where the time goes in v3:
time: 152 us; the launch traced here: 151 us
  Pallas kernels  150 us (99%)
    pallas_call x1, Pallas kernels, gram_rows(): pl.pallas_call(gram_kernel, out_shape=(pltpu.VMEM((kk, cols), F32), pltpu...  150 us

profile of v3, /device:TPU:0, one launch (start us, length us, event | category | flops | bytes accessed | tf_op | source)
XLA Modules:
  0.0 151.4 jit_solution(10382799153948356296)
XLA Ops:
  0.0 0.0 copy-start
  0.0 150.4 %gram_rows.1 = (f32[512,512]{1,0:T(8,128)S(1)}, s32[1,1]{1,0:T(1,128)S(4)}) custom-call(f32[6144,512]{1,0:T(8,128)} %a_hbm.1, f32[4,128]{1,0:T(4,128)} %s_hbm.1), custom_call_target="tpu_custom_call" | custom-call | tf_op jit(solution)/shard_map/gram_rows/pallas_call | solution.py:466
  150.4 0.0 copy-done
  150.4 1.0 copy.66
  (1 shorter events, 0.0 us)
Async XLA Ops:
  0.0 150.4 %copy-start = (f32[4,128]{1,0:T(4,128)S(1)}, f32[4,128]{1,0:T(4,128)}, u32[]{:S(2)}) copy-start(f32[4,128]{1,0:T(4,128)} %s_hbm.1) | copy-start | bytes 6148

commit v4 on v3

--- a/solution.py
+++ b/solution.py
@@ -179,8 +179,8 @@
         state = state[:n - done] + state[half:half + n - done]
 
 
-def gram_kernel(a_hbm, s_hbm, r_ref, ok_ref, s_ref, w_buf, y_buf, acc1, acc2, acc1_r, h_buf, cm_buf, cm_recv, cy_recv, cfin,
-                xp, xp_r, tail_r, tail_s, last_buf, z_buf, t_buf, rf_buf, k12, ymax, u_blk, m_blk,
+def gram_kernel(a_hbm, s_hbm, r_ref, ok_ref, s_ref, own, peer, acc1, acc2, acc1_r, hb, cm_buf, cm_recv, cy_recv, cfin,
+                xp, xp_r, tail_r, tail_s, done_s, done_r, z_buf, t_buf, rf_buf, k12, ymax, u_blk, m_blk,
                 load_sem, ya_send, ya_recv, yb_send, yb_recv, ar_send, ar_recv, gy_send, gy_recv, gq_send, gq_recv,
                 rs_send, rs_recv, cy_send, cy_rsem, ag_send, ag_recv, s_sem):
     rows, cols = a_hbm.shape
@@ -190,22 +190,30 @@
     c = lax.axis_index('pcol')
     p = lax.axis_index('prow')
     other = 1 - c
-    core_peer = p + 1 - 2 * (p % 2)
+    core = p % 2
+    core_peer = p + 1 - 2 * core
     x_peer = (p + 2) % 4
     qr = half // 4
+    qb = NB // 4
     ca = 512
     n_a = half_rows // ca
-    b_cuts = ((0, 768, 1920, 3072), (0, 1024, 2048, 2816, 3072))
+    n_l = rows // ca
+    per_load = n_l // 4
+    b_cuts = ((0, 768, 1920, 3072), (0, 1024, 2048, 2944, 3072))
     n_b = [len(cuts) - 1 for cuts in b_cuts]
-    n_l = rows // ca
 
     def row0(start, size):
         return pl.ds(pl.multiple_of(start, NB), size)
 
-    def load(j):
-        rs = pl.ds(pl.multiple_of(j * ca, ca), ca)
-        return (pltpu.make_async_copy(a_hbm.at[rs, pl.ds(0, half)], w_buf.at[c, rs, :], load_sem.at[0, j]),
-                pltpu.make_async_copy(a_hbm.at[rs, pl.ds(half, half)], y_buf.at[rs, :], load_sem.at[1, j]))
+    def to_prow(src, dst, send, recv, q):
+        return pltpu.make_async_remote_copy(src, dst, send, recv, device_id={'prow': q}, device_id_type=MESH)
+
+    def to_pcol(src, dst, send, recv):
+        return pltpu.make_async_remote_copy(src, dst, send, recv, device_id={'pcol': other}, device_id_type=MESH)
+
+    def load(g):
+        rs = row0(g * per_load * ca, per_load * ca)
+        return pltpu.make_async_copy(a_hbm.at[rs, :], own.at[rs, :], load_sem.at[g])
 
     barrier = pltpu.get_barrier_semaphore()
     pl.semaphore_signal(barrier, inc=1, device_id={'pcol': other}, device_id_type=MESH)
@@ -213,33 +221,32 @@
         pl.semaphore_signal(barrier, inc=1, device_id={'prow': (p + d) % 4}, device_id_type=MESH)
     s_load = pltpu.make_async_copy(s_hbm, s_ref, s_sem)
     s_load.start()
-    for j in range(n_l):
-        for cp in load(j):
-            cp.start()
+    for g in range(4):
+        load(g).start()
     pl.semaphore_wait(barrier, 4)
 
+    def send_rows(start, size, lanes, send, recv):
+        rs = row0(start, size)
+        return to_pcol(a_hbm.at[rs, lanes], peer.at[rs, lanes], send, recv)
+
     def send_a(k):
-        rs = row0(c * half_rows + k * ca, ca)
-        return pltpu.make_async_remote_copy(a_hbm.at[rs, pl.ds(0, half)], w_buf.at[c, rs, :], ya_send.at[k], ya_recv.at[k],
-                                            device_id={'pcol': other}, device_id_type=MESH)
+        return send_rows(c * half_rows + k * ca, ca, pl.ds(0, half), ya_send, ya_recv.at[k])
 
     def send_b(l, k):
-        rs = row0(other * half_rows + b_cuts[l][k], b_cuts[l][k + 1] - b_cuts[l][k])
-        ls = pl.ds(l * NB, NB)
-        return pltpu.make_async_remote_copy(a_hbm.at[rs, ls], w_buf.at[c, rs, ls], yb_send.at[l, k], yb_recv.at[l, k],
-                                            device_id={'pcol': other}, device_id_type=MESH)
+        lo, hi = b_cuts[l][k], b_cuts[l][k + 1]
+        return send_rows(other * half_rows + lo, hi - lo, pl.ds(l * NB, NB), yb_send.at[l], yb_recv.at[l, k])
 
     for k in range(4):
         send_a(k).start()
 
     eye = (lax.broadcasted_iota(jnp.int32, (NB, NB), 0) == lax.broadcasted_iota(jnp.int32, (NB, NB), 1)).astype(F32)
 
-    def add_shift(side, l, cond):
+    def add_shift(ref, side, l, cond):
         @pl.when(jnp.logical_and(p == 0, cond))
         def _():
             panel = 2 * l + side
             rs = row0(panel * NB, NB)
-            w_buf[side, rs, l * NB:(l + 1) * NB] = w_buf[side, rs, l * NB:(l + 1) * NB] + eye * s_ref[pl.ds(panel, 1), :]
+            ref[rs, l * NB:(l + 1) * NB] = ref[rs, l * NB:(l + 1) * NB] + eye * s_ref[pl.ds(panel, 1), :]
 
     acc1[...] = jnp.zeros_like(acc1)
     acc2[...] = jnp.zeros_like(acc2)
@@ -248,18 +255,21 @@
 
     @pl.loop(0, n_l)
     def _(j):
-        for cp in load(j):
-            cp.wait()
+        @pl.when(j % per_load == 0)
+        def _():
+            load(j // per_load).wait()
+
         for l in range(2):
-            add_shift(c, l, j == 0)
+            add_shift(own, c, l, j == 0)
         rs = pl.ds(pl.multiple_of(j * ca, ca), ca)
-        left = w_buf[c, rs, :]
-        right = y_buf[rs, :]
-        ymax[...] = jnp.maximum(ymax[...], jnp.max(jnp.abs(right).reshape(ca // 8, 8, half), axis=0))
-        acc1[...] += dot_tn(left, jnp.concatenate([left, right], axis=1))
-
-    def pair_copy(src, dst, slot, peer):
-        return pltpu.make_async_remote_copy(src, dst, ar_send.at[slot], ar_recv.at[slot], device_id={'prow': peer}, device_id_type=MESH)
+        right = own[rs, :]
+        ymax[...] = jnp.maximum(ymax[...], jnp.max(jnp.abs(right[:, half:]).reshape(ca // 8, 8, half), axis=0))
+        acc1[...] += dot_tn(right[:, :half], right)
+
+    acc1[NB:NB + 8, :NB] = jnp.maximum(ymax[:, :NB], ymax[:, NB:])
+
+    def pair_copy(src, dst, slot, q):
+        return to_prow(src, dst, ar_send.at[slot], ar_recv.at[slot], q)
 
     g1 = pair_copy(acc1, acc1_r.at[0], 0, core_peer)
     g1.start()
@@ -269,27 +279,30 @@
     g2.start()
     g2.wait()
     acc1[...] += acc1_r[1]
-    h_buf[c] = acc1[:, :half]
-    quarter = pl.ds(pl.multiple_of(p * qr, qr), qr)
-    gy = pltpu.make_async_remote_copy(h_buf.at[c, quarter, :], h_buf.at[c, quarter, :], gy_send, gy_recv,
-                                      device_id={'pcol': other}, device_id_type=MESH)
+    for q in range(4):
+        rs = slice(q * qb, (q + 1) * qb)
+        hb[c, q, :qb, :] = acc1[rs, :NB]
+        hb[c, q, qb:2 * qb, :] = acc1[rs, NB:half]
+        hb[c, q, 2 * qb:3 * qb, :] = acc1[NB + q * qb:NB + (q + 1) * qb, NB:half]
+        hb[c, q, 3 * qb:, :] = acc1[NB:NB + 8, :NB]
+    gy = to_pcol(hb.at[c, p], hb.at[c, p], gy_send, gy_recv)
     gy.start()
     for k in range(4, n_a):
         send_a(k).start()
     send_b(0, 0).start()
 
+    def gram_block(side, b):
+        return jnp.concatenate([hb[side, q, b * qb:(b + 1) * qb, :] for q in range(4)], axis=0)
+
     def take_a(k):
         send_a(k).wait_recv()
         for l in range(2):
-            add_shift(other, l, jnp.logical_and(c == 1, k == 0))
+            add_shift(peer, other, l, jnp.logical_and(c == 1, k == 0))
         rs = row0(other * half_rows + k * ca, ca)
-        right = jnp.concatenate([w_buf[c, rs, :], y_buf[rs, :]], axis=1)
-        acc2[...] += dot_tn(w_buf[other, rs, :], right)
+        acc2[...] += dot_tn(peer[rs, :], own[rs, :])
 
     def spread_gram(d, src):
-        rs = pl.ds(pl.multiple_of(src * qr, qr), qr)
-        return pltpu.make_async_remote_copy(h_buf.at[other, rs, :], h_buf.at[other, rs, :], gq_send.at[d], gq_recv.at[d],
-                                            device_id={'prow': (p + d) % 4}, device_id_type=MESH)
+        return to_prow(hb.at[other, src], hb.at[other, src], gq_send.at[d - 1], gq_recv.at[d - 1], (p + d) % 4)
 
     @pl.loop(0, n_a)
     def _(k):
@@ -306,26 +319,22 @@
             for d in range(1, 4):
                 spread_gram(d, p).wait_send()
                 spread_gram(d, (p + 4 - d) % 4).wait_recv()
-            factor_block(h_buf[0, :NB, :NB], u_blk, m_blk)
+            factor_block(gram_block(0, 0), u_blk, m_blk)
 
     @pl.when(c == 0)
     def _():
         ct = acc2[:, :half].T
         for q in range(4):
-            cm_buf[q, :qr, :] = ct[q * qr:(q + 1) * qr]
+            cm_buf[q] = ct[q * qr:(q + 1) * qr]
 
     @pl.when(c == 1)
     def _():
         for q in range(4):
-            cm_buf[q, :qr, :] = acc2[q * qr:(q + 1) * qr, :half]
-
-    for q in range(4):
-        cm_buf[q, qr:, :] = ymax[...]
+            cm_buf[q] = acc2[q * qr:(q + 1) * qr, :half]
 
     def scatter(d):
         q = (p + d) % 4
-        return pltpu.make_async_remote_copy(cm_buf.at[q], cm_recv.at[d - 1], rs_send.at[d], rs_recv.at[d],
-                                            device_id={'prow': q}, device_id_type=MESH)
+        return to_prow(cm_buf.at[q], cm_recv.at[d - 1], rs_send.at[d - 1], rs_recv.at[d - 1], q)
 
     for d in range(1, 4):
         scatter(d).start()
@@ -334,7 +343,7 @@
     for d in range(1, 4):
         scatter(d).wait()
     cm_buf[p] = ((cm_buf[p] + cm_recv[0]) + cm_recv[1]) + cm_recv[2]
-    cy = pltpu.make_async_remote_copy(cm_buf.at[p], cy_recv, cy_send, cy_rsem, device_id={'pcol': other}, device_id_type=MESH)
+    cy = to_pcol(cm_buf.at[p], cy_recv, cy_send, cy_rsem)
     cy.start()
     for k in range(1, n_b[0]):
         send_b(0, k).start()
@@ -344,17 +353,15 @@
     cfin[p] = cm_buf[p] + cy_recv[...]
 
     def spread(d, src):
-        return pltpu.make_async_remote_copy(cfin.at[src], cfin.at[src], ag_send.at[d], ag_recv.at[d],
-                                            device_id={'prow': (p + d) % 4}, device_id_type=MESH)
+        return to_prow(cfin.at[src], cfin.at[src], ag_send.at[d - 1], ag_recv.at[d - 1], (p + d) % 4)
 
     for d in range(1, 4):
         spread(d, p).start()
-
     for d in range(1, 4):
         spread(d, p).wait_send()
         spread(d, (p + 4 - d) % 4).wait_recv()
 
-    cross = jnp.concatenate([cfin[q, :qr, :] for q in range(4)], axis=0)
+    cross = jnp.concatenate([cfin[q] for q in range(4)], axis=0)
     z_buf[...] = jnp.zeros_like(z_buf)
     diag_max = jnp.zeros((1, NB), F32)
     diag_min = jnp.full((1, NB), jnp.inf, F32)
@@ -364,7 +371,7 @@
         for j in range(i, 4):
             cj, lj = j % 2, j // 2
             if ci == cj:
-                block = h_buf[ci, li * NB:(li + 1) * NB, lj * NB:(lj + 1) * NB]
+                block = gram_block(ci, li + lj)
             elif ci == 0:
                 block = cross[li * NB:(li + 1) * NB, lj * NB:(lj + 1) * NB]
             else:
@@ -402,7 +409,8 @@
     total = jnp.sum(trace, axis=1, keepdims=True)
     d_max = jnp.max(diag_max, axis=1, keepdims=True)
     d_min = jnp.min(diag_min, axis=1, keepdims=True)
-    y_max = jnp.max(jnp.max(cfin[0, qr:, :], axis=0, keepdims=True), axis=1, keepdims=True)
+    y_max = jnp.maximum(hb[0, 0, 3 * qb:, :], hb[1, 0, 3 * qb:, :])
+    y_max = jnp.max(jnp.max(y_max, axis=0, keepdims=True), axis=1, keepdims=True)
     good = (total < TRACE_FACTOR * kk) & (d_min > 1e-26) & (d_max < 1e36) & (y_max * jnp.sqrt(d_max) < 1e33)
     ok_ref[0, 0] = jnp.where(good, 1, 0)[0, 0]
 
@@ -417,9 +425,9 @@
     def take_b(l, k):
         send_b(l, k).wait_recv()
         if k == 0:
-            add_shift(other, l, c == 0)
+            add_shift(peer, other, l, c == 0)
         rs = row0(c * half_rows + b_cuts[l][k], b_cuts[l][k + 1] - b_cuts[l][k])
-        xp[l] += dot_tn(w_buf[other, rs, l * NB:(l + 1) * NB], y_buf[rs, :])
+        xp[l] += dot_tn(peer[rs, l * NB:(l + 1) * NB], own[rs, half:])
 
     for k in range(n_b[0]):
         take_b(0, k)
@@ -434,26 +442,27 @@
     r_ref[:, half:] = dot_nn(t_buf[...], k12[...])
     for k in range(n_b[1]):
         take_b(1, k)
-    mine = pl.ds(pl.multiple_of((p % 2) * (NB // 2), NB // 2), NB // 2)
-    theirs = pl.ds(pl.multiple_of((1 - p % 2) * (NB // 2), NB // 2), NB // 2)
-    x3 = pair_copy(xp.at[1, theirs, :], tail_r.at[0], 4, core_peer)
+    mine = pl.ds(pl.multiple_of(core * NB, NB), NB)
+    theirs = pl.ds(pl.multiple_of((1 - core) * NB, NB), NB)
+    x3 = pair_copy(xp.at[1, :, theirs], tail_r.at[0], 4, core_peer)
     x3.start()
     x3.wait()
-    tail_s[...] = xp[1, mine, :] + tail_r[0]
+    tail_s[...] = xp[1, :, mine] + tail_r[0]
     x4 = pair_copy(tail_s, tail_r.at[1], 5, x_peer)
     x4.start()
     x4.wait()
-    last_buf[mine, :] = tail_s[...] + tail_r[1]
-    x5 = pair_copy(last_buf.at[mine, :], last_buf.at[mine, :], 6, core_peer)
+    r_mine = pl.ds(pl.multiple_of(half + core * NB, NB), NB)
+    r_theirs = pl.ds(pl.multiple_of(half + (1 - core) * NB, NB), NB)
+    inv_cols = t_buf[half:, pl.ds(pl.multiple_of((3 - c) * NB, NB), NB)]
+    done_s[...] = r_ref[half:, r_mine] + dot_nn(inv_cols, tail_s[...] + tail_r[1])
+    x5 = pair_copy(done_s, done_r, 6, core_peer)
     x5.start()
+    r_ref[half:, r_mine] = done_s[...]
+    send_rows(c * half_rows, half_rows, pl.ds(0, half), ya_send, ya_recv.at[0]).wait_send()
+    for l in range(2):
+        send_rows(other * half_rows, half_rows, pl.ds(l * NB, NB), yb_send.at[l], yb_recv.at[l, 0]).wait_send()
     x5.wait()
-    r_ref[half:, half:] += dot_nn(t_buf[half:, pl.ds(pl.multiple_of((3 - c) * NB, NB), NB)], last_buf[...])
-
-    for k in range(n_a):
-        send_a(k).wait_send()
-    for l in range(2):
-        for k in range(n_b[l]):
-            send_b(l, k).wait_send()
+    r_ref[half:, r_theirs] = done_r[...]
 
 
 def gram_rows(a_loc, diag_shift):
@@ -469,14 +478,12 @@
         in_specs=[pl.BlockSpec(memory_space=pl.ANY), pl.BlockSpec(memory_space=pl.ANY)],
         out_specs=(pl.BlockSpec(memory_space=pltpu.VMEM), pl.BlockSpec(memory_space=pltpu.SMEM)),
         scratch_shapes=[
-            vm(*diag_shift.shape),
-            vm(2, rows, half), vm(rows, half), vm(half, cols), vm(half, cols), vm(2, half, cols), vm(2, half, half),
-            vm(4, qr + 8, half), vm(3, qr + 8, half), vm(qr + 8, half), vm(4, qr + 8, half),
-            vm(2, NB, half), vm(2, NB, half), vm(2, NB // 2, half), vm(NB // 2, half), vm(NB, half), vm(kk, kk), vm(kk, kk), vm(kk, kk), vm(kk, half), vm(8, half),
-            vm(NB, NB), vm(NB, NB),
-            dma((2, rows // 512)), dma((rows // 1024,)), dma((rows // 1024,)), dma((2, 4)), dma((2, 4)),
-            dma((7,)), dma((7,)), dma, dma, dma((4,)), dma((4,)),
-            dma((4,)), dma((4,)), dma, dma, dma((4,)), dma((4,)), dma,
+            vm(*diag_shift.shape), vm(rows, cols), vm(rows, half), vm(half, cols), vm(half, cols), vm(2, half, cols),
+            vm(2, 4, 3 * NB // 4 + 8, NB), vm(4, qr, half), vm(3, qr, half), vm(qr, half), vm(4, qr, half),
+            vm(2, NB, half), vm(2, NB, half), vm(2, NB, NB), vm(NB, NB), vm(half, NB), vm(half, NB),
+            vm(kk, kk), vm(kk, kk), vm(kk, kk), vm(kk, half), vm(8, half), vm(NB, NB), vm(NB, NB),
+            dma((4,)), dma, dma((rows // 1024,)), dma((2,)), dma((2, 4)), dma((7,)), dma((7,)), dma, dma, dma((3,)), dma((3,)),
+            dma((3,)), dma((3,)), dma, dma, dma((3,)), dma((3,)), dma,
         ],
         compiler_params=pltpu.CompilerParams(collective_id=0, has_side_effects=True, vmem_limit_bytes=48 * 1024 * 1024),
         name='gram_rows',

time: 152 us -> 151 us (level)
  no operation moved by 1% of the time
where the time goes in v4:
time: 151 us
  Pallas kernels  150 us (99%)
    pallas_call x1, Pallas kernels, gram_rows(): pl.pallas_call(gram_kernel, out_shape=(pltpu.VMEM((kk, cols), F32), pltpu...  150 us

profile of v4, /device:TPU:0, one launch (start us, length us, event | category | flops | bytes accessed | tf_op | source)
XLA Modules:
  0.0 150.6 jit_solution(10750539462076689149)
XLA Ops:
  0.0 0.0 copy-start
  0.0 149.6 %gram_rows.1 = (f32[512,512]{1,0:T(8,128)S(1)}, s32[1,1]{1,0:T(1,128)S(4)}) custom-call(f32[6144,512]{1,0:T(8,128)} %a_hbm.1, f32[4,128]{1,0:T(4,128)} %s_hbm.1), custom_call_target="tpu_custom_call" | custom-call | tf_op jit(solution)/shard_map/gram_rows/pallas_call | solution.py:475
  149.6 0.0 copy-done
  149.6 1.0 copy.66
  (1 shorter events, 0.0 us)
Async XLA Ops:
  0.0 149.6 %copy-start = (f32[4,128]{1,0:T(4,128)S(1)}, f32[4,128]{1,0:T(4,128)}, u32[]{:S(2)}) copy-start(f32[4,128]{1,0:T(4,128)} %s_hbm.1) | copy-start | bytes 6148

commit v5 on v4

--- a/solution.py
+++ b/solution.py
@@ -98,14 +98,15 @@
         is_owner = col_id == owner_col
         panel = lax.dynamic_slice_in_dim(a_loc, start_col, blocksize, axis=1)
         factored, vectors, tau_vec, sign_vec = factor_panel(panel, glob_rows, panel_idx * blocksize)
-        gram_mat = gather_sum(jnp.einsum('mi,mj->ij', vectors, vectors, precision=PRECISE, preferred_element_type=F32), 'prow')
-        t_factor = build_tfactor(gram_mat, tau_vec)
-        vectors, t_factor, sign_vec = owned(vectors, is_owner), owned(t_factor, is_owner), owned(sign_vec, is_owner)
+        vectors, scalars = owned(vectors, is_owner), owned(jnp.stack([tau_vec, sign_vec]), is_owner)
+        tau_vec, sign_vec = scalars[0], scalars[1]
         signs = lax.dynamic_update_slice_in_dim(signs, sign_vec, panel_idx * blocksize, axis=0)
         keep_cols = orig_cols >= (panel_idx + 1) * blocksize
-        proj = jnp.einsum('mi,mn->in', vectors, a_loc, precision=PRECISE, preferred_element_type=F32)
-        quarter = cols_loc // 4
-        proj_sum = jnp.concatenate([gather_sum(proj[:, q * quarter:(q + 1) * quarter], 'prow') for q in range(4)], axis=1)
+        proj = jnp.einsum('mi,mn->in', vectors, jnp.concatenate([vectors, a_loc], axis=1), precision=PRECISE, preferred_element_type=F32)
+        pieces = cols_loc // blocksize + 1
+        sums = lax.map(lambda x: gather_sum(x, 'prow'), jnp.swapaxes(proj.reshape(blocksize, pieces, blocksize), 0, 1))
+        t_factor = build_tfactor(sums[0], tau_vec)
+        proj_sum = jnp.swapaxes(sums[1:], 0, 1).reshape(blocksize, cols_loc)
         w_mat = jnp.where(keep_cols[None, :], jnp.einsum('ij,in->jn', t_factor, proj_sum, precision=PRECISE, preferred_element_type=F32), 0.0)
         a_loc = a_loc - jnp.dot(vectors, w_mat, precision=PRECISE, preferred_element_type=F32)
         kept = lax.dynamic_slice_in_dim(a_loc, start_col, blocksize, axis=1)
@@ -179,9 +180,9 @@
         state = state[:n - done] + state[half:half + n - done]
 
 
-def gram_kernel(a_hbm, s_hbm, r_ref, ok_ref, s_ref, own, peer, acc1, acc2, acc1_r, hb, cm_buf, cm_recv, cy_recv, cfin,
-                xp, xp_r, tail_r, tail_s, done_s, done_r, z_buf, t_buf, rf_buf, k12, ymax, u_blk, m_blk,
-                load_sem, ya_send, ya_recv, yb_send, yb_recv, ar_send, ar_recv, gy_send, gy_recv, gq_send, gq_recv,
+def gram_kernel(a_hbm, s_hbm, r_ref, ok_ref, s_ref, own, peer, pack, pack_r, acc1, acc2, acc1_r, hb, cm_buf, cm_recv, cy_recv, cfin,
+                xp, xp_r, xg, xg_r, k_first, k_last, tail_r, tail_s, done_s, done_r, z_buf, t_buf, rf_buf, k12, ymax, u_blk, m_blk,
+                load_sem, ya_send, ya_recv, yb_send, yb_recv, yp_send, yp_recv, ar_send, ar_recv, gy_send, gy_recv, gq_send, gq_recv,
                 rs_send, rs_recv, cy_send, cy_rsem, ag_send, ag_recv, s_sem):
     rows, cols = a_hbm.shape
     half_rows = rows // 2
@@ -199,8 +200,13 @@
     n_a = half_rows // ca
     n_l = rows // ca
     per_load = n_l // 4
-    b_cuts = ((0, 768, 1920, 3072), (0, 1024, 2048, 2944, 3072))
-    n_b = [len(cuts) - 1 for cuts in b_cuts]
+    b_cuts = (0, 768, 1920, 3072)
+    n_b = len(b_cuts) - 1
+    n_g = 4
+    wg = NB // n_g
+    rq = half_rows // n_g
+    last_cuts = (0, 512, 640, 704, 768)
+    p_cuts = [(g, 0, rq) for g in range(n_g - 1)] + [(n_g - 1, lo, hi) for lo, hi in zip(last_cuts, last_cuts[1:])]
 
     def row0(start, size):
         return pl.ds(pl.multiple_of(start, NB), size)
@@ -232,9 +238,13 @@
     def send_a(k):
         return send_rows(c * half_rows + k * ca, ca, pl.ds(0, half), ya_send, ya_recv.at[k])
 
-    def send_b(l, k):
-        lo, hi = b_cuts[l][k], b_cuts[l][k + 1]
-        return send_rows(other * half_rows + lo, hi - lo, pl.ds(l * NB, NB), yb_send.at[l], yb_recv.at[l, k])
+    def send_b(k):
+        lo, hi = b_cuts[k], b_cuts[k + 1]
+        return send_rows(other * half_rows + lo, hi - lo, pl.ds(0, NB), yb_send, yb_recv.at[k])
+
+    def send_p(i):
+        g, lo, hi = p_cuts[i]
+        return to_pcol(pack.at[g, pl.ds(lo, hi - lo), :], pack_r.at[g, pl.ds(lo, hi - lo), :], yp_send, yp_recv.at[i])
 
     for k in range(4):
         send_a(k).start()
@@ -277,6 +287,20 @@
     acc1[...] += acc1_r[0]
     g2 = pair_copy(acc1, acc1_r.at[1], 1, x_peer)
     g2.start()
+
+    group_of = lax.broadcasted_iota(jnp.int32, (rq // 8, NB), 1) // wg
+
+    @pl.loop(0, 8)
+    def _(i):
+        step = rq // 8
+        parts = [own[pl.ds(pl.multiple_of(other * half_rows + q * rq + i * step, 8), step), NB:half] for q in range(n_g)]
+        for g in range(n_g):
+            packed = jnp.zeros((step, NB), F32)
+            for q in range(n_g):
+                turn = wg * ((q - g) % n_g)
+                packed = jnp.where(group_of == q, pltpu.roll(parts[q], turn, 1) if turn else parts[q], packed)
+            pack[g, pl.ds(pl.multiple_of(i * step, 8), step), :] = packed
+
     g2.wait()
     acc1[...] += acc1_r[1]
     for q in range(4):
@@ -289,7 +313,7 @@
     gy.start()
     for k in range(4, n_a):
         send_a(k).start()
-    send_b(0, 0).start()
+    send_b(0).start()
 
     def gram_block(side, b):
         return jnp.concatenate([hb[side, q, b * qb:(b + 1) * qb, :] for q in range(4)], axis=0)
@@ -338,17 +362,20 @@
 
     for d in range(1, 4):
         scatter(d).start()
-    for l in range(2):
-        xp[l] = acc2[l * NB:(l + 1) * NB, half:]
+    xp[...] = acc2[:NB, half:]
+    for g in range(n_g):
+        xg[g] = acc2[NB + g * wg:NB + (g + 1) * wg, half:]
+    k_first[...] = jnp.zeros_like(k_first)
+    k_last[...] = jnp.zeros_like(k_last)
     for d in range(1, 4):
         scatter(d).wait()
     cm_buf[p] = ((cm_buf[p] + cm_recv[0]) + cm_recv[1]) + cm_recv[2]
     cy = to_pcol(cm_buf.at[p], cy_recv, cy_send, cy_rsem)
     cy.start()
-    for k in range(1, n_b[0]):
-        send_b(0, k).start()
-    for k in range(n_b[1]):
-        send_b(1, k).start()
+    for k in range(1, n_b):
+        send_b(k).start()
+    for i in range(len(p_cuts)):
+        send_p(i).start()
     cy.wait()
     cfin[p] = cm_buf[p] + cy_recv[...]
 
@@ -422,46 +449,68 @@
     k12[row0((c + 2) * NB, NB), :] = acc1[NB:, half:]
     k12[row0((3 - c) * NB, NB), :] = jnp.zeros((NB, half), F32)
 
-    def take_b(l, k):
-        send_b(l, k).wait_recv()
+    for k in range(n_b):
+        send_b(k).wait_recv()
         if k == 0:
-            add_shift(peer, other, l, c == 0)
-        rs = row0(c * half_rows + b_cuts[l][k], b_cuts[l][k + 1] - b_cuts[l][k])
-        xp[l] += dot_tn(peer[rs, l * NB:(l + 1) * NB], own[rs, half:])
-
-    for k in range(n_b[0]):
-        take_b(0, k)
-    x1 = pair_copy(xp.at[0], xp_r.at[0], 2, core_peer)
+            add_shift(peer, other, 0, c == 0)
+        rs = row0(c * half_rows + b_cuts[k], b_cuts[k + 1] - b_cuts[k])
+        xp[...] += dot_tn(peer[rs, :NB], own[rs, half:])
+    x1 = pair_copy(xp, xp_r.at[0], 2, core_peer)
     x1.start()
     x1.wait()
-    xp[0] = xp[0] + xp_r[0]
-    x2 = pair_copy(xp.at[0], xp_r.at[1], 3, x_peer)
+    xp[...] = xp[...] + xp_r[0]
+    x2 = pair_copy(xp, xp_r.at[1], 3, x_peer)
     x2.start()
     x2.wait()
-    k12[row0((1 - c) * NB, NB), :] = xp[0] + xp_r[1]
+    k12[row0((1 - c) * NB, NB), :] = xp[...] + xp_r[1]
     r_ref[:, half:] = dot_nn(t_buf[...], k12[...])
-    for k in range(n_b[1]):
-        take_b(1, k)
+
+    def take_p(g, lo, hi):
+        turned = pack_r[g, lo:hi, :].T
+        for q in range(n_g):
+            rs = pl.ds(pl.multiple_of(c * half_rows + q * rq + lo, 8), hi - lo)
+            xg[g] += dot_nn(turned[q * wg:(q + 1) * wg, :], own[rs, half:])
+
+    inv_cols = t_buf[half:, pl.ds(pl.multiple_of((3 - c) * NB, NB), NB)]
+
+    @pl.loop(0, n_g - 1)
+    def _(g):
+        to_pcol(pack.at[g], pack_r.at[g], yp_send, yp_recv.at[g]).wait_recv()
+        take_p(g, 0, rq)
+        x3 = pair_copy(xg.at[g], xg_r.at[0, g], 4 + 2 * g, core_peer)
+        x3.start()
+        x3.wait()
+        xg[g] = xg[g] + xg_r[0, g]
+        x4 = pair_copy(xg.at[g], xg_r.at[1, g], 5 + 2 * g, x_peer)
+        x4.start()
+        x4.wait()
+        k_first[pl.ds(pl.multiple_of(g * wg, wg), wg), :] = xg[g] + xg_r[1, g]
+
+    r_ref[half:, half:] += dot_nn(inv_cols, k_first[...])
+    for i in range(n_g - 1, len(p_cuts)):
+        send_p(i).wait_recv()
+        take_p(*p_cuts[i])
+    g = n_g - 1
     mine = pl.ds(pl.multiple_of(core * NB, NB), NB)
     theirs = pl.ds(pl.multiple_of((1 - core) * NB, NB), NB)
-    x3 = pair_copy(xp.at[1, :, theirs], tail_r.at[0], 4, core_peer)
-    x3.start()
-    x3.wait()
-    tail_s[...] = xp[1, :, mine] + tail_r[0]
-    x4 = pair_copy(tail_s, tail_r.at[1], 5, x_peer)
-    x4.start()
-    x4.wait()
+    x5 = pair_copy(xg.at[g, :, theirs], tail_r.at[0], 10, core_peer)
+    x5.start()
+    x5.wait()
+    tail_s[...] = xg[g, :, mine] + tail_r[0]
+    x6 = pair_copy(tail_s, tail_r.at[1], 11, x_peer)
+    x6.start()
+    x6.wait()
+    k_last[g * wg:, :] = tail_s[...] + tail_r[1]
     r_mine = pl.ds(pl.multiple_of(half + core * NB, NB), NB)
     r_theirs = pl.ds(pl.multiple_of(half + (1 - core) * NB, NB), NB)
-    inv_cols = t_buf[half:, pl.ds(pl.multiple_of((3 - c) * NB, NB), NB)]
-    done_s[...] = r_ref[half:, r_mine] + dot_nn(inv_cols, tail_s[...] + tail_r[1])
-    x5 = pair_copy(done_s, done_r, 6, core_peer)
-    x5.start()
+    done_s[...] = r_ref[half:, r_mine] + dot_nn(inv_cols, k_last[...])
+    x7 = pair_copy(done_s, done_r, 12, core_peer)
+    x7.start()
     r_ref[half:, r_mine] = done_s[...]
     send_rows(c * half_rows, half_rows, pl.ds(0, half), ya_send, ya_recv.at[0]).wait_send()
-    for l in range(2):
-        send_rows(other * half_rows, half_rows, pl.ds(l * NB, NB), yb_send.at[l], yb_recv.at[l, 0]).wait_send()
-    x5.wait()
+    send_rows(other * half_rows, half_rows, pl.ds(0, NB), yb_send, yb_recv.at[0]).wait_send()
+    to_pcol(pack, pack_r, yp_send, yp_recv.at[0]).wait_send()
+    x7.wait()
     r_ref[half:, r_theirs] = done_r[...]
 
 
@@ -478,11 +527,12 @@
         in_specs=[pl.BlockSpec(memory_space=pl.ANY), pl.BlockSpec(memory_space=pl.ANY)],
         out_specs=(pl.BlockSpec(memory_space=pltpu.VMEM), pl.BlockSpec(memory_space=pltpu.SMEM)),
         scratch_shapes=[
-            vm(*diag_shift.shape), vm(rows, cols), vm(rows, half), vm(half, cols), vm(half, cols), vm(2, half, cols),
+            vm(*diag_shift.shape), vm(rows, cols), vm(rows, half), vm(4, rows // 8, NB), vm(4, rows // 8, NB), vm(half, cols), vm(half, cols), vm(2, half, cols),
             vm(2, 4, 3 * NB // 4 + 8, NB), vm(4, qr, half), vm(3, qr, half), vm(qr, half), vm(4, qr, half),
-            vm(2, NB, half), vm(2, NB, half), vm(2, NB, NB), vm(NB, NB), vm(half, NB), vm(half, NB),
+            vm(NB, half), vm(2, NB, half), vm(4, NB // 4, half), vm(2, 3, NB // 4, half), vm(NB, half), vm(NB, NB),
+            vm(2, NB // 4, NB), vm(NB // 4, NB), vm(half, NB), vm(half, NB),
             vm(kk, kk), vm(kk, kk), vm(kk, kk), vm(kk, half), vm(8, half), vm(NB, NB), vm(NB, NB),
-            dma((4,)), dma, dma((rows // 1024,)), dma((2,)), dma((2, 4)), dma((7,)), dma((7,)), dma, dma, dma((3,)), dma((3,)),
+            dma((4,)), dma, dma((rows // 1024,)), dma, dma((3,)), dma, dma((7,)), dma((13,)), dma((13,)), dma, dma, dma((3,)), dma((3,)),
             dma((3,)), dma((3,)), dma, dma, dma((3,)), dma((3,)), dma,
         ],
         compiler_params=pltpu.CompilerParams(collective_id=0, has_side_effects=True, vmem_limit_bytes=48 * 1024 * 1024),

time: 151 us -> 150 us (level)
  no operation moved by 1% of the time
where the time goes in v5:
time: 150 us
  Pallas kernels  149 us (99%)
    pallas_call x1, Pallas kernels, gram_rows(): pl.pallas_call(gram_kernel, out_shape=(pltpu.VMEM((kk, cols), F32), pltpu...  149 us

profile of v5, /device:TPU:0, one launch (start us, length us, event | category | flops | bytes accessed | tf_op | source)
XLA Modules:
  0.0 150.0 jit_solution(17220801470407427783)
XLA Ops:
  0.0 0.0 copy-start
  0.0 149.0 %gram_rows.1 = (f32[512,512]{1,0:T(8,128)S(1)}, s32[1,1]{1,0:T(1,128)S(4)}) custom-call(f32[6144,512]{1,0:T(8,128)} %a_hbm.1, f32[4,128]{1,0:T(4,128)} %s_hbm.1), custom_call_target="tpu_custom_call" | custom-call | tf_op jit(solution)/shard_map/gram_rows/pallas_call | solution.py:524
  149.0 0.0 copy-done
  149.0 1.0 copy.88
  (1 shorter events, 0.0 us)
Async XLA Ops:
  0.0 149.0 %copy-start = (f32[4,128]{1,0:T(4,128)S(1)}, f32[4,128]{1,0:T(4,128)}, u32[]{:S(2)}) copy-start(f32[4,128]{1,0:T(4,128)} %s_hbm.1) | copy-start | bytes 6148

commit v6 on v5

--- a/solution.py
+++ b/solution.py
@@ -180,9 +180,9 @@
         state = state[:n - done] + state[half:half + n - done]
 
 
-def gram_kernel(a_hbm, s_hbm, r_ref, ok_ref, s_ref, own, peer, pack, pack_r, acc1, acc2, acc1_r, hb, cm_buf, cm_recv, cy_recv, cfin,
-                xp, xp_r, xg, xg_r, k_first, k_last, tail_r, tail_s, done_s, done_r, z_buf, t_buf, rf_buf, k12, ymax, u_blk, m_blk,
-                load_sem, ya_send, ya_recv, yb_send, yb_recv, yp_send, yp_recv, ar_send, ar_recv, gy_send, gy_recv, gq_send, gq_recv,
+def gram_kernel(a_hbm, s_hbm, r_ref, ok_ref, s_ref, own, peer, pack, pack_r, fine, fine_r, acc1, acc2, acc1_r, hb, cm_buf, cm_recv, cy_recv, cfin,
+                xp, xp_r, xc, xt, z_buf, t_buf, rf_buf, k12, ymax, u_blk, m_blk,
+                load_sem, ya_send, ya_recv, yb_send, yb_recv, yp_send, yp_recv, yf_send, yf_recv, fs_send, fs_recv, ar_send, ar_recv, gy_send, gy_recv, gq_send, gq_recv,
                 rs_send, rs_recv, cy_send, cy_rsem, ag_send, ag_recv, s_sem):
     rows, cols = a_hbm.shape
     half_rows = rows // 2
@@ -205,8 +205,10 @@
     n_g = 4
     wg = NB // n_g
     rq = half_rows // n_g
-    last_cuts = (0, 512, 640, 704, 768)
-    p_cuts = [(g, 0, rq) for g in range(n_g - 1)] + [(n_g - 1, lo, hi) for lo, hi in zip(last_cuts, last_cuts[1:])]
+    n_f = 2 * n_g
+    wf = NB // n_f
+    rf = half_rows // n_f
+    f_cuts = [(0, 0, rf)] + [(1, lo, hi) for lo, hi in ((0, 256), (256, 352), (352, rf))]
 
     def row0(start, size):
         return pl.ds(pl.multiple_of(start, NB), size)
@@ -242,9 +244,12 @@
         lo, hi = b_cuts[k], b_cuts[k + 1]
         return send_rows(other * half_rows + lo, hi - lo, pl.ds(0, NB), yb_send, yb_recv.at[k])
 
-    def send_p(i):
-        g, lo, hi = p_cuts[i]
-        return to_pcol(pack.at[g, pl.ds(lo, hi - lo), :], pack_r.at[g, pl.ds(lo, hi - lo), :], yp_send, yp_recv.at[i])
+    def send_p(g):
+        return to_pcol(pack.at[g], pack_r.at[g], yp_send, yp_recv.at[g])
+
+    def send_f(i):
+        g, lo, hi = f_cuts[i]
+        return to_pcol(fine.at[g, pl.ds(lo, hi - lo), :], fine_r.at[g, pl.ds(lo, hi - lo), :], yf_send, yf_recv.at[i])
 
     for k in range(4):
         send_a(k).start()
@@ -288,19 +293,25 @@
     g2 = pair_copy(acc1, acc1_r.at[1], 1, x_peer)
     g2.start()
 
-    group_of = lax.broadcasted_iota(jnp.int32, (rq // 8, NB), 1) // wg
-
-    @pl.loop(0, 8)
-    def _(i):
-        step = rq // 8
-        parts = [own[pl.ds(pl.multiple_of(other * half_rows + q * rq + i * step, 8), step), NB:half] for q in range(n_g)]
-        for g in range(n_g):
-            packed = jnp.zeros((step, NB), F32)
-            for q in range(n_g):
-                turn = wg * ((q - g) % n_g)
-                packed = jnp.where(group_of == q, pltpu.roll(parts[q], turn, 1) if turn else parts[q], packed)
-            pack[g, pl.ds(pl.multiple_of(i * step, 8), step), :] = packed
-
+    def pack_groups(dst, count, first):
+        width = NB // count
+        depth = half_rows // count
+        step = depth // 8
+        group_of = lax.broadcasted_iota(jnp.int32, (step, NB), 1) // width
+
+        @pl.loop(0, 8)
+        def _(i):
+            packed = [jnp.zeros((step, NB), F32) for _ in range(dst.shape[0])]
+            for q in range(count):
+                part = own[pl.ds(pl.multiple_of(other * half_rows + q * depth + i * step, 8), step), NB:half]
+                for g in range(dst.shape[0]):
+                    turn = width * ((q - g - first) % count)
+                    packed[g] = jnp.where(group_of == q, pltpu.roll(part, turn, 1) if turn else part, packed[g])
+            for g in range(dst.shape[0]):
+                dst[g, pl.ds(pl.multiple_of(i * step, 8), step), :] = packed[g]
+
+    pack_groups(pack, n_g, 0)
+    pack_groups(fine, n_f, n_f - 2)
     g2.wait()
     acc1[...] += acc1_r[1]
     for q in range(4):
@@ -363,10 +374,7 @@
     for d in range(1, 4):
         scatter(d).start()
     xp[...] = acc2[:NB, half:]
-    for g in range(n_g):
-        xg[g] = acc2[NB + g * wg:NB + (g + 1) * wg, half:]
-    k_first[...] = jnp.zeros_like(k_first)
-    k_last[...] = jnp.zeros_like(k_last)
+    xc[...] = acc2[NB:, half:]
     for d in range(1, 4):
         scatter(d).wait()
     cm_buf[p] = ((cm_buf[p] + cm_recv[0]) + cm_recv[1]) + cm_recv[2]
@@ -374,8 +382,10 @@
     cy.start()
     for k in range(1, n_b):
         send_b(k).start()
-    for i in range(len(p_cuts)):
-        send_p(i).start()
+    for g in range(n_g - 1):
+        send_p(g).start()
+    for i in range(len(f_cuts)):
+        send_f(i).start()
     cy.wait()
     cfin[p] = cm_buf[p] + cy_recv[...]
 
@@ -465,53 +475,46 @@
     k12[row0((1 - c) * NB, NB), :] = xp[...] + xp_r[1]
     r_ref[:, half:] = dot_nn(t_buf[...], k12[...])
 
-    def take_p(g, lo, hi):
-        turned = pack_r[g, lo:hi, :].T
-        for q in range(n_g):
-            rs = pl.ds(pl.multiple_of(c * half_rows + q * rq + lo, 8), hi - lo)
-            xg[g] += dot_nn(turned[q * wg:(q + 1) * wg, :], own[rs, half:])
-
-    inv_cols = t_buf[half:, pl.ds(pl.multiple_of((3 - c) * NB, NB), NB)]
+    def take_packed(block, base, depth, start, count, width):
+        rs = pl.ds(pl.multiple_of(start, 8), width)
+        turned = block.T
+        total = xc[rs, :]
+        for q in range(count):
+            ys = pl.ds(pl.multiple_of(c * half_rows + q * depth + base, 8), block.shape[0])
+            total = total + dot_nn(turned[q * width:(q + 1) * width, :], own[ys, half:])
+        xc[rs, :] = total
+
+    def share(d, start, size, last):
+        rs = pl.ds(pl.multiple_of(start, 8), size)
+        return to_prow(xc.at[rs, :], xt.at[p, rs, :], fs_send.at[d - 1], fs_recv.at[last, d - 1], (p + d) % 4)
 
     @pl.loop(0, n_g - 1)
     def _(g):
-        to_pcol(pack.at[g], pack_r.at[g], yp_send, yp_recv.at[g]).wait_recv()
-        take_p(g, 0, rq)
-        x3 = pair_copy(xg.at[g], xg_r.at[0, g], 4 + 2 * g, core_peer)
-        x3.start()
-        x3.wait()
-        xg[g] = xg[g] + xg_r[0, g]
-        x4 = pair_copy(xg.at[g], xg_r.at[1, g], 5 + 2 * g, x_peer)
-        x4.start()
-        x4.wait()
-        k_first[pl.ds(pl.multiple_of(g * wg, wg), wg), :] = xg[g] + xg_r[1, g]
-
-    r_ref[half:, half:] += dot_nn(inv_cols, k_first[...])
-    for i in range(n_g - 1, len(p_cuts)):
-        send_p(i).wait_recv()
-        take_p(*p_cuts[i])
-    g = n_g - 1
-    mine = pl.ds(pl.multiple_of(core * NB, NB), NB)
-    theirs = pl.ds(pl.multiple_of((1 - core) * NB, NB), NB)
-    x5 = pair_copy(xg.at[g, :, theirs], tail_r.at[0], 10, core_peer)
-    x5.start()
-    x5.wait()
-    tail_s[...] = xg[g, :, mine] + tail_r[0]
-    x6 = pair_copy(tail_s, tail_r.at[1], 11, x_peer)
-    x6.start()
-    x6.wait()
-    k_last[g * wg:, :] = tail_s[...] + tail_r[1]
-    r_mine = pl.ds(pl.multiple_of(half + core * NB, NB), NB)
-    r_theirs = pl.ds(pl.multiple_of(half + (1 - core) * NB, NB), NB)
-    done_s[...] = r_ref[half:, r_mine] + dot_nn(inv_cols, k_last[...])
-    x7 = pair_copy(done_s, done_r, 12, core_peer)
-    x7.start()
-    r_ref[half:, r_mine] = done_s[...]
+        send_p(g).wait_recv()
+        take_packed(pack_r[g], 0, rq, g * wg, n_g, wg)
+        for d in range(1, 4):
+            share(d, g * wg, wg, 0).start()
+
+    inv_cols = t_buf[half:, pl.ds(pl.multiple_of((3 - c) * NB, NB), NB)]
+    for i in range(len(f_cuts)):
+        g, lo, hi = f_cuts[i]
+        start = NB - 2 * wf + g * wf
+        send_f(i).wait_recv()
+        take_packed(fine_r[g, lo:hi, :], lo, rf, start, n_f, wf)
+        if hi == rf:
+            for d in range(1, 4):
+                share(d, start, wf, g).start()
+    xt[p] = xc[...]
     send_rows(c * half_rows, half_rows, pl.ds(0, half), ya_send, ya_recv.at[0]).wait_send()
     send_rows(other * half_rows, half_rows, pl.ds(0, NB), yb_send, yb_recv.at[0]).wait_send()
     to_pcol(pack, pack_r, yp_send, yp_recv.at[0]).wait_send()
-    x7.wait()
-    r_ref[half:, r_theirs] = done_r[...]
+    to_pcol(fine, fine_r, yf_send, yf_recv.at[0]).wait_send()
+    for d in range(1, 4):
+        share(d, 0, NB, 0).wait_send()
+        share(d, 0, NB - wf, 0).wait_recv()
+    for d in range(1, 4):
+        share(d, NB - wf, wf, 1).wait_recv()
+    r_ref[half:, half:] += dot_nn(inv_cols, (xt[0] + xt[1]) + (xt[2] + xt[3]))
 
 
 def gram_rows(a_loc, diag_shift):
@@ -527,12 +530,11 @@
         in_specs=[pl.BlockSpec(memory_space=pl.ANY), pl.BlockSpec(memory_space=pl.ANY)],
         out_specs=(pl.BlockSpec(memory_space=pltpu.VMEM), pl.BlockSpec(memory_space=pltpu.SMEM)),
         scratch_shapes=[
-            vm(*diag_shift.shape), vm(rows, cols), vm(rows, half), vm(4, rows // 8, NB), vm(4, rows // 8, NB), vm(half, cols), vm(half, cols), vm(2, half, cols),
+            vm(*diag_shift.shape), vm(rows, cols), vm(rows, half), vm(3, rows // 8, NB), vm(3, rows // 8, NB), vm(2, rows // 16, NB), vm(2, rows // 16, NB), vm(half, cols), vm(half, cols), vm(2, half, cols),
             vm(2, 4, 3 * NB // 4 + 8, NB), vm(4, qr, half), vm(3, qr, half), vm(qr, half), vm(4, qr, half),
-            vm(NB, half), vm(2, NB, half), vm(4, NB // 4, half), vm(2, 3, NB // 4, half), vm(NB, half), vm(NB, NB),
-            vm(2, NB // 4, NB), vm(NB // 4, NB), vm(half, NB), vm(half, NB),
+            vm(NB, half), vm(2, NB, half), vm(NB, half), vm(4, NB, half),
             vm(kk, kk), vm(kk, kk), vm(kk, kk), vm(kk, half), vm(8, half), vm(NB, NB), vm(NB, NB),
-            dma((4,)), dma, dma((rows // 1024,)), dma, dma((3,)), dma, dma((7,)), dma((13,)), dma((13,)), dma, dma, dma((3,)), dma((3,)),
+            dma((4,)), dma, dma((rows // 1024,)), dma, dma((3,)), dma, dma((3,)), dma, dma((4,)), dma((3,)), dma((2, 3)), dma((4,)), dma((4,)), dma, dma, dma((3,)), dma((3,)),
             dma((3,)), dma((3,)), dma, dma, dma((3,)), dma((3,)), dma,
         ],
         compiler_params=pltpu.CompilerParams(collective_id=0, has_side_effects=True, vmem_limit_bytes=48 * 1024 * 1024),

time: 150 us -> 150 us (level)
  no operation moved by 1% of the time
where the time goes in v6:
time: 150 us; the launch traced here: 149 us
  Pallas kernels  148 us (99%)
    pallas_call x1, Pallas kernels, gram_rows(): pl.pallas_call(gram_kernel, out_shape=(pltpu.VMEM((kk, cols), F32), pltpu...  148 us

profile of v6, /device:TPU:0, one launch (start us, length us, event | category | flops | bytes accessed | tf_op | source)
XLA Modules:
  0.0 149.5 jit_solution(8192179284736729599)
XLA Ops:
  0.0 0.0 copy-start
  0.0 148.4 %gram_rows.1 = (f32[512,512]{1,0:T(8,128)S(1)}, s32[1,1]{1,0:T(1,128)S(4)}) custom-call(f32[6144,512]{1,0:T(8,128)} %a_hbm.1, f32[4,128]{1,0:T(4,128)} %s_hbm.1), custom_call_target="tpu_custom_call" | custom-call | tf_op jit(solution)/shard_map/gram_rows/pallas_call | solution.py:527
  148.5 0.0 copy-done
  148.5 1.0 copy.88
  (1 shorter events, 0.0 us)
Async XLA Ops:
  0.0 148.5 %copy-start = (f32[4,128]{1,0:T(4,128)S(1)}, f32[4,128]{1,0:T(4,128)}, u32[]{:S(2)}) copy-start(f32[4,128]{1,0:T(4,128)} %s_hbm.1) | copy-start | bytes 6148

commit v7 on v6

--- a/solution.py
+++ b/solution.py
@@ -180,9 +180,9 @@
         state = state[:n - done] + state[half:half + n - done]
 
 
-def gram_kernel(a_hbm, s_hbm, r_ref, ok_ref, s_ref, own, peer, pack, pack_r, fine, fine_r, acc1, acc2, acc1_r, hb, cm_buf, cm_recv, cy_recv, cfin,
+def gram_kernel(a_hbm, s_hbm, r_ref, ok_ref, s_ref, own, peer, turned, turned_r, acc1, acc2, acc1_r, hb, cm_buf, cm_recv, cy_recv, cfin,
                 xp, xp_r, xc, xt, z_buf, t_buf, rf_buf, k12, ymax, u_blk, m_blk,
-                load_sem, ya_send, ya_recv, yb_send, yb_recv, yp_send, yp_recv, yf_send, yf_recv, fs_send, fs_recv, ar_send, ar_recv, gy_send, gy_recv, gq_send, gq_recv,
+                load_sem, ya_send, ya_recv, yb_send, yb_recv, yp_send, yp_recv, fs_send, fs_recv, ar_send, ar_recv, gy_send, gy_recv, gq_send, gq_recv,
                 rs_send, rs_recv, cy_send, cy_rsem, ag_send, ag_recv, s_sem):
     rows, cols = a_hbm.shape
     half_rows = rows // 2
@@ -202,13 +202,11 @@
     per_load = n_l // 4
     b_cuts = (0, 768, 1920, 3072)
     n_b = len(b_cuts) - 1
-    n_g = 4
-    wg = NB // n_g
-    rq = half_rows // n_g
-    n_f = 2 * n_g
-    wf = NB // n_f
-    rf = half_rows // n_f
-    f_cuts = [(0, 0, rf)] + [(1, lo, hi) for lo, hi in ((0, 256), (256, 352), (352, rf))]
+    starts = (0, 64, 112, NB)
+    last_rows = (0, 1536, 2560, 3072)
+    pieces = [(lo, hi - lo, 0, half_rows) for lo, hi in zip(starts[:-2], starts[1:-1])]
+    pieces += [(starts[-2], NB - starts[-2], lo, hi - lo) for lo, hi in zip(last_rows, last_rows[1:])]
+    tail = starts[-2]
 
     def row0(start, size):
         return pl.ds(pl.multiple_of(start, NB), size)
@@ -244,12 +242,10 @@
         lo, hi = b_cuts[k], b_cuts[k + 1]
         return send_rows(other * half_rows + lo, hi - lo, pl.ds(0, NB), yb_send, yb_recv.at[k])
 
-    def send_p(g):
-        return to_pcol(pack.at[g], pack_r.at[g], yp_send, yp_recv.at[g])
-
-    def send_f(i):
-        g, lo, hi = f_cuts[i]
-        return to_pcol(fine.at[g, pl.ds(lo, hi - lo), :], fine_r.at[g, pl.ds(lo, hi - lo), :], yf_send, yf_recv.at[i])
+    def send_p(i):
+        col, width, lo, depth = pieces[i]
+        block = (pl.ds(col, width), pl.ds(lo, depth))
+        return to_pcol(turned.at[block], turned_r.at[block], yp_send, yp_recv.at[i])
 
     for k in range(4):
         send_a(k).start()
@@ -293,25 +289,10 @@
     g2 = pair_copy(acc1, acc1_r.at[1], 1, x_peer)
     g2.start()
 
-    def pack_groups(dst, count, first):
-        width = NB // count
-        depth = half_rows // count
-        step = depth // 8
-        group_of = lax.broadcasted_iota(jnp.int32, (step, NB), 1) // width
-
-        @pl.loop(0, 8)
-        def _(i):
-            packed = [jnp.zeros((step, NB), F32) for _ in range(dst.shape[0])]
-            for q in range(count):
-                part = own[pl.ds(pl.multiple_of(other * half_rows + q * depth + i * step, 8), step), NB:half]
-                for g in range(dst.shape[0]):
-                    turn = width * ((q - g - first) % count)
-                    packed[g] = jnp.where(group_of == q, pltpu.roll(part, turn, 1) if turn else part, packed[g])
-            for g in range(dst.shape[0]):
-                dst[g, pl.ds(pl.multiple_of(i * step, 8), step), :] = packed[g]
-
-    pack_groups(pack, n_g, 0)
-    pack_groups(fine, n_f, n_f - 2)
+    @pl.loop(0, half_rows // NB)
+    def _(i):
+        turned[:, row0(i * NB, NB)] = own[row0(other * half_rows + i * NB, NB), NB:half].T
+
     g2.wait()
     acc1[...] += acc1_r[1]
     for q in range(4):
@@ -382,10 +363,8 @@
     cy.start()
     for k in range(1, n_b):
         send_b(k).start()
-    for g in range(n_g - 1):
-        send_p(g).start()
-    for i in range(len(f_cuts)):
-        send_f(i).start()
+    for i in range(len(pieces)):
+        send_p(i).start()
     cy.wait()
     cfin[p] = cm_buf[p] + cy_recv[...]
 
@@ -475,45 +454,42 @@
     k12[row0((1 - c) * NB, NB), :] = xp[...] + xp_r[1]
     r_ref[:, half:] = dot_nn(t_buf[...], k12[...])
 
-    def take_packed(block, base, depth, start, count, width):
-        rs = pl.ds(pl.multiple_of(start, 8), width)
-        turned = block.T
-        total = xc[rs, :]
-        for q in range(count):
-            ys = pl.ds(pl.multiple_of(c * half_rows + q * depth + base, 8), block.shape[0])
-            total = total + dot_nn(turned[q * width:(q + 1) * width, :], own[ys, half:])
-        xc[rs, :] = total
+    def take_p(i):
+        col, width, lo, depth = pieces[i]
+        send_p(i).wait_recv()
+        step = min(depth, 1024)
+
+        def part(start):
+            xc[col:col + width, :] += dot_nn(turned_r[col:col + width, row0(start, step)], own[row0(c * half_rows + start, step), half:])
+
+        if depth % step:
+            step = depth // 3
+        if depth == step:
+            part(lo)
+        else:
+            @pl.loop(0, depth // step)
+            def _(j):
+                part(lo + j * step)
 
     def share(d, start, size, last):
         rs = pl.ds(pl.multiple_of(start, 8), size)
         return to_prow(xc.at[rs, :], xt.at[p, rs, :], fs_send.at[d - 1], fs_recv.at[last, d - 1], (p + d) % 4)
 
-    @pl.loop(0, n_g - 1)
-    def _(g):
-        send_p(g).wait_recv()
-        take_packed(pack_r[g], 0, rq, g * wg, n_g, wg)
-        for d in range(1, 4):
-            share(d, g * wg, wg, 0).start()
-
     inv_cols = t_buf[half:, pl.ds(pl.multiple_of((3 - c) * NB, NB), NB)]
-    for i in range(len(f_cuts)):
-        g, lo, hi = f_cuts[i]
-        start = NB - 2 * wf + g * wf
-        send_f(i).wait_recv()
-        take_packed(fine_r[g, lo:hi, :], lo, rf, start, n_f, wf)
-        if hi == rf:
+    for i, (col, width, lo, depth) in enumerate(pieces):
+        take_p(i)
+        if lo + depth == half_rows:
             for d in range(1, 4):
-                share(d, start, wf, g).start()
+                share(d, col, width, int(col == tail)).start()
     xt[p] = xc[...]
     send_rows(c * half_rows, half_rows, pl.ds(0, half), ya_send, ya_recv.at[0]).wait_send()
     send_rows(other * half_rows, half_rows, pl.ds(0, NB), yb_send, yb_recv.at[0]).wait_send()
-    to_pcol(pack, pack_r, yp_send, yp_recv.at[0]).wait_send()
-    to_pcol(fine, fine_r, yf_send, yf_recv.at[0]).wait_send()
+    to_pcol(turned, turned_r, yp_send, yp_recv.at[0]).wait_send()
     for d in range(1, 4):
         share(d, 0, NB, 0).wait_send()
-        share(d, 0, NB - wf, 0).wait_recv()
-    for d in range(1, 4):
-        share(d, NB - wf, wf, 1).wait_recv()
+        share(d, 0, tail, 0).wait_recv()
+    for d in range(1, 4):
+        share(d, tail, NB - tail, 1).wait_recv()
     r_ref[half:, half:] += dot_nn(inv_cols, (xt[0] + xt[1]) + (xt[2] + xt[3]))
 
 
@@ -530,11 +506,11 @@
         in_specs=[pl.BlockSpec(memory_space=pl.ANY), pl.BlockSpec(memory_space=pl.ANY)],
         out_specs=(pl.BlockSpec(memory_space=pltpu.VMEM), pl.BlockSpec(memory_space=pltpu.SMEM)),
         scratch_shapes=[
-            vm(*diag_shift.shape), vm(rows, cols), vm(rows, half), vm(3, rows // 8, NB), vm(3, rows // 8, NB), vm(2, rows // 16, NB), vm(2, rows // 16, NB), vm(half, cols), vm(half, cols), vm(2, half, cols),
+            vm(*diag_shift.shape), vm(rows, cols), vm(rows, half), vm(NB, rows // 2), vm(NB, rows // 2), vm(half, cols), vm(half, cols), vm(2, half, cols),
             vm(2, 4, 3 * NB // 4 + 8, NB), vm(4, qr, half), vm(3, qr, half), vm(qr, half), vm(4, qr, half),
             vm(NB, half), vm(2, NB, half), vm(NB, half), vm(4, NB, half),
             vm(kk, kk), vm(kk, kk), vm(kk, kk), vm(kk, half), vm(8, half), vm(NB, NB), vm(NB, NB),
-            dma((4,)), dma, dma((rows // 1024,)), dma, dma((3,)), dma, dma((3,)), dma, dma((4,)), dma((3,)), dma((2, 3)), dma((4,)), dma((4,)), dma, dma, dma((3,)), dma((3,)),
+            dma((4,)), dma, dma((rows // 1024,)), dma, dma((3,)), dma, dma((7,)), dma((3,)), dma((2, 3)), dma((4,)), dma((4,)), dma, dma, dma((3,)), dma((3,)),
             dma((3,)), dma((3,)), dma, dma, dma((3,)), dma((3,)), dma,
         ],
         compiler_params=pltpu.CompilerParams(collective_id=0, has_side_effects=True, vmem_limit_bytes=48 * 1024 * 1024),

time: 150 us -> 148 us (0.987)
  no operation moved by 1% of the time
where the time goes in v7:
time: 148 us
  Pallas kernels  147 us (99%)
    pallas_call x1, Pallas kernels, gram_rows(): pl.pallas_call(gram_kernel, out_shape=(pltpu.VMEM((kk, cols), F32), pltpu...  147 us

profile of v7, /device:TPU:0, one launch (start us, length us, event | category | flops | bytes accessed | tf_op | source)
XLA Modules:
  0.0 148.3 jit_solution(9966356284825398654)
XLA Ops:
  0.0 0.0 copy-start
  0.0 147.3 %gram_rows.1 = (f32[512,512]{1,0:T(8,128)S(1)}, s32[1,1]{1,0:T(1,128)S(4)}) custom-call(f32[6144,512]{1,0:T(8,128)} %a_hbm.1, f32[4,128]{1,0:T(4,128)} %s_hbm.1), custom_call_target="tpu_custom_call" | custom-call | tf_op jit(solution)/shard_map/gram_rows/pallas_call | solution.py:503
  147.3 0.0 copy-done
  147.3 1.0 copy.88
  (1 shorter events, 0.0 us)
Async XLA Ops:
  0.0 147.3 %copy-start = (f32[4,128]{1,0:T(4,128)S(1)}, f32[4,128]{1,0:T(4,128)}, u32[]{:S(2)}) copy-start(f32[4,128]{1,0:T(4,128)} %s_hbm.1) | copy-start | bytes 6148
